TPU v7x, 32 devices: a whole 2x2x4 slice. The times are simulated.
32 devices in a mesh: segment: 4 (over y, x), amp: 8 (over z, core).
Axes of the slice: x: 2, y: 2, z: 4, core: 2. Of those that a mesh axis runs over, the one named last changes fastest.
Arguments:
- states: float32 [4, 2097152], P('segment', 'amp'), may hold values from -6 to 6
- gate_blocks: float32 [4, 3, 128, 128], P('segment'), may hold values from -1 to 1, as said below
- kraus_picks: int32 [4, 4, 3, 7], P('segment'), may hold values from 0 to 3
- block_targets: int32 [4, 3], replicated, may hold values from 0 to 1
Outputs:
- final_states: float32 [4, 2097152], P('segment', 'amp')
- log_weights: float32 [4, 4], P('segment')
Inputs may be any that keep to these rules, and one draw needn't show every extreme that they name: Every block of gate_blocks is an orthogonal matrix, up to rounding.
All inputs are finite; a program needn't handle non-finite values.
Results may differ from a plain program's by a relative error of at most 0.0003.
Values sent between devices are 32-bit elements; how exact they have to be, the bound alone decides.
No kernel may reach another device: no remote copies, remote signals or barrier semaphores. Data moves between devices by JAX's collectives and lax.ppermute only.
A program may use at most 64 MiB of HBM per device.

v0:
```python
import functools

import jax
import jax.numpy as jnp
from jax import lax
from jax.experimental import pallas as pl
from jax.experimental.pallas import tpu as pltpu
from jax.sharding import PartitionSpec as P


KEEP_FACTORS = (1.0, 0.9, 1.0, 0.97)
FLIP_FACTORS = (0.9, 1.0, 0.97, 1.0)
F32 = jnp.float32
BF16 = jnp.bfloat16
VMEM = pl.BlockSpec(memory_space=pltpu.VMEM)
SMEM = pl.BlockSpec(memory_space=pltpu.SMEM)
EXTRA = 8
VMEM_LIMIT = 12 * 2**20


def split(value):
    high = value.astype(BF16)
    return high, (value - high.astype(F32)).astype(BF16)


def pack_kernel(x_ref, *out_refs):
    me = lax.axis_index("amp")
    register, middle, lanes = x_ref.shape
    rows = x_ref.reshape(register * middle, lanes)
    for far, out in enumerate(out_refs):
        for near in range(2):
            out[near] = rows[pl.ds(me ^ (2 * far + near), register, stride=middle), :]


def pack_both_kernel(x_ref, side_ref, *out_refs):
    me = lax.axis_index("amp")
    register, middle, lanes = x_ref.shape
    for near, ref in enumerate((x_ref, side_ref)):
        rows = ref.reshape(register * middle, lanes)
        for far, out in enumerate(out_refs):
            out[near] = rows[pl.ds(me ^ (2 * far), register, stride=middle), :]


def part_kernel(*refs):
    lines = len(refs) - 2
    for far in range(lines):
        refs[lines][far] = refs[far][0]
        refs[lines + 1][far] = refs[far][1]


def join_kernel(own_ref, other_ref, *out_refs):
    for far, out in enumerate(out_refs):
        out[0] = own_ref[far]
        out[1] = other_ref[far]


def pick_of(pick, factors):
    value = jnp.float32(factors[-1])
    for option in range(len(factors) - 1):
        value = jnp.where(pick == option, factors[option], value)
    return value


def noise_rows(picks_ref, section, block, register):
    rows = lax.broadcasted_iota(jnp.int32, (register, register), 0)
    product = jnp.ones((register, register), F32)
    qubits = picks_ref.shape[-1]
    for q in range(qubits):
        pick = picks_ref[section, block, q]
        bit = jnp.right_shift(rows, qubits - 1 - q) & 1
        product = product * jnp.where(bit == 1, pick_of(pick, FLIP_FACTORS), pick_of(pick, KEEP_FACTORS))
    return product


def combine_kernel(sections, picks_ref, targets_ref, *refs):
    gate_refs, (low_ref, high_ref) = refs[:sections], refs[sections:]
    seg = lax.axis_index("segment")
    blocks, register = gate_refs[0].shape[0], gate_refs[0].shape[-1]
    rows = lax.broadcasted_iota(jnp.int32, (register, register), 0)
    columns = lax.broadcasted_iota(jnp.int32, (register, register), 1)
    eye = (rows == columns).astype(F32)
    zero = jnp.zeros((register, register), BF16)
    for k in range(sections):
        section = seg ^ k
        low, high = eye, eye
        for block in range(blocks):
            on_low = targets_ref[section, block] == 0
            moved = gate_refs[k][block] * noise_rows(picks_ref, section, block, register)
            if block > 0:
                before = jnp.where(on_low, low, high)
                moved = jnp.dot(moved, before, precision=lax.Precision.HIGHEST, preferred_element_type=F32)
            low, high = jnp.where(on_low, moved, low), jnp.where(on_low, high, moved)
        big, small = split(low.T)
        low_ref[section] = jnp.concatenate(
            [jnp.concatenate([big, small], axis=1), jnp.concatenate([big, zero], axis=1)], axis=0
        )
        big, small = split(high)
        high_ref[section] = jnp.concatenate(
            [jnp.concatenate([big, big], axis=1), jnp.concatenate([small, zero], axis=1)], axis=0
        )


def on_low(value, weights):
    lanes = value.shape[1]
    both = jnp.dot(jnp.concatenate(split(value), axis=1), weights, preferred_element_type=F32)
    return both[:, :lanes] + both[:, lanes:]


def on_high(value, weights):
    rows = value.shape[0] // 2
    wide = jnp.concatenate([value[:rows], value[rows:]], axis=1)
    both = jnp.dot(weights, jnp.concatenate(split(wide), axis=0), preferred_element_type=F32)
    both = both[:rows] + both[rows:]
    lanes = value.shape[1]
    return jnp.concatenate([both[:, :lanes], both[:, lanes:]], axis=0)


def piece_of(refs, far, near):
    return refs[near].at[far] if len(refs) == 2 else refs[far].at[near]


def sections_kernel(sections, lines, pieces, last, *refs):
    amp = 2 * lines
    piece_refs, (low_ref, high_ref) = refs[:pieces], refs[pieces : pieces + 2]
    at = pieces + 2
    if last:
        sums_in, at = refs[at], at + 1
    out_refs, x = refs[at:-1], refs[-1]
    me = lax.axis_index("amp")
    register, lanes = piece_refs[0].shape[-2:]
    rest = register // amp

    def squares(total, value):
        return total + jnp.sum(value * value, axis=0, keepdims=True)

    total = jnp.zeros((1, lanes), F32)
    for far in range(lines):
        for near in range(2):
            value = piece_of(piece_refs, far, near)[...]
            total = squares(total, value)
            x[me ^ (2 * far + near)] = value
    sums = [total]
    for section in range(sections):
        low, high = low_ref[section], high_ref[section]
        total = jnp.zeros((1, lanes), F32)
        for pair in range(lines):
            parts = (2 * pair, 2 * pair + 1)
            if section % 2 == 0:
                value = jnp.concatenate([x[part] for part in parts], axis=0)
            else:
                spans = [x[:, part * rest : (part + 1) * rest, :].reshape(register, lanes) for part in parts]
                value = jnp.concatenate(spans, axis=0)
            value = on_high(on_low(value, low), high)
            total = squares(total, value)
            for half, part in enumerate(parts):
                piece = value[half * register : (half + 1) * register]
                if section % 2 == 0:
                    x[part] = piece
                else:
                    x[:, part * rest : (part + 1) * rest, :] = piece.reshape(amp, rest, lanes)
        sums.append(total)
    rows = jnp.concatenate(sums + [jnp.zeros((EXTRA - len(sums), lanes), F32)], axis=0)
    if last:
        rows = rows + sums_in[...]
    else:
        out_refs[lines][...] = rows
    for far in range(lines):
        for near in range(2):
            out = piece_of(out_refs if last else out_refs[:lines], far, near)
            out[0:register, :] = x[me ^ (2 * far + near)]
            if last:
                out[register:, :] = rows


def unpack_kernel(lines, counts, total_amps, *refs):
    held = []
    for count in counts:
        held, refs = held + [refs[:count]], refs[count:]
    x_ref, logs_ref = refs
    me = lax.axis_index("amp")
    register, middle, lanes = x_ref.shape
    sections = logs_ref.shape[1]
    totals = jnp.zeros((EXTRA, lanes), F32)
    for far in range(lines):
        for near in range(2):
            totals = totals + piece_of(held[-1], far, near)[register:, :]
    totals = jnp.sum(totals, axis=1, keepdims=True)
    logs = jnp.log(totals[1 : sections + 1] / totals[:sections])
    rows = lax.broadcasted_iota(jnp.int32, (sections, sections), 0)
    columns = lax.broadcasted_iota(jnp.int32, (sections, sections), 1)
    logs_ref[...] = jnp.sum(jnp.where(rows == columns, logs, 0.0), axis=0, keepdims=True)
    scale = 1.0 / jnp.sqrt(totals[sections : sections + 1] / total_amps)
    out = x_ref.reshape(register * middle, lanes)
    for chunk, pieces in enumerate(held):
        for far in range(lines):
            for near in range(2):
                value = piece_of(pieces, far, near)[0:register, :]
                m = chunk * 2 * lines + (me ^ (2 * far + near))
                out[pl.ds(m, register, stride=middle), :] = value * scale


def swap(piece, k, size, axis):
    if k == 0:
        return piece
    return lax.ppermute(piece, axis, [(i, i ^ k) for i in range(size)])


def body_fast(states, gate_blocks, kraus_picks, block_targets):
    amp_local = states.shape[1]
    register = gate_blocks.shape[-1]
    amp, sections = lax.axis_size("amp"), lax.axis_size("segment")
    middle = amp_local // (register * register)
    chunks, lines = middle // amp, amp // 2
    params = pltpu.CompilerParams(vmem_limit_bytes=VMEM_LIMIT)

    def array(*shape, dtype=F32):
        return jax.ShapeDtypeStruct(shape, dtype)

    def kernel(body, out_shape, *operands, in_specs=None, **options):
        specs = dict(in_specs=in_specs or [VMEM] * len(operands))
        if "grid" not in options:
            specs["out_specs"] = [VMEM] * len(out_shape)
        return pl.pallas_call(body, out_shape=out_shape, compiler_params=params, **specs, **options)(*operands)

    def along(pieces):
        back = {far: swap(pieces[far], 2 * far, amp, "amp") for far in range(lines - 1, -1, -1)}
        return [back[far] for far in range(lines)]

    def across(piece):
        return swap(piece, 1, amp, "amp")

    pairs, halves = [array(2, register, register)] * lines, [array(lines, register, register)] * 2
    x = states.reshape(register, middle, register)
    arrived = []
    for chunk in range(chunks):
        if chunk == 0:
            packed = kernel(
                pack_kernel,
                pairs,
                pltpu.with_memory_space_constraint(x, pltpu.HBM),
                grid=(1,),
                in_specs=[pl.BlockSpec((register, amp, register), lambda i: (0, 0, 0))],
                out_specs=[pl.BlockSpec((2, register, register), lambda i: (0, 0, 0))] * lines,
            )
            near, other = kernel(part_kernel, halves, *along(packed))
            arrived.append([near, across(other)])
        else:
            own = x[:, chunk * amp : (chunk + 1) * amp, :]
            packed = kernel(pack_both_kernel, pairs, own, across(own))
            arrived.append(along(packed))

    gates = [swap(gate_blocks[0], k, sections, "segment") for k in range(sections)]
    low, high = kernel(
        functools.partial(combine_kernel, sections),
        [array(sections, 2 * register, 2 * register, dtype=BF16)] * 2,
        kraus_picks[0],
        block_targets,
        *gates,
        in_specs=[SMEM, SMEM] + [VMEM] * sections,
    )

    carried, held = [], []
    for chunk, pieces in enumerate(arrived):
        last = chunk == chunks - 1
        results = kernel(
            functools.partial(sections_kernel, sections, lines, len(pieces), last),
            [array(lines, register + EXTRA, register)] * 2 if last else pairs + [array(EXTRA, register)],
            *pieces,
            low,
            high,
            *carried,
            scratch_shapes=[pltpu.VMEM((amp, register, register), F32)],
        )
        if last:
            own, other = results
            tall = [array(2, register + EXTRA, register)] * lines
            joined = kernel(join_kernel, tall, own, across(other))
            held.append(along(joined))
        else:
            carried = [results[lines]]
            near, other = kernel(part_kernel, halves, *along(results[:lines]))
            held.append([near, across(other)])

    out, logs = kernel(
        functools.partial(unpack_kernel, lines, [len(pieces) for pieces in held], float(amp_local * amp)),
        [array(register, middle, register), array(1, sections)],
        *[piece for pieces in held for piece in pieces],
    )
    return out.reshape(1, amp_local), logs


def noise_factors(kraus_rows):
    qubit_count = kraus_rows.shape[-1]
    register = 2**qubit_count
    positions = jnp.arange(register, dtype=jnp.int32)
    product = jnp.ones(kraus_rows.shape[:-1] + (register,), jnp.float32)
    for qubit_pos in range(qubit_count):
        bit_value = jnp.right_shift(positions, qubit_count - 1 - qubit_pos) & 1
        column = kraus_rows[..., qubit_pos : qubit_pos + 1]
        low_value = jnp.zeros(column.shape, jnp.float32)
        high_value = jnp.zeros(column.shape, jnp.float32)
        for option in range(4):
            picked = (column == option).astype(jnp.float32)
            low_value = low_value + picked * KEEP_FACTORS[option]
            high_value = high_value + picked * FLIP_FACTORS[option]
        product = product * jnp.where(bit_value == 1, high_value, low_value)
    return product


def apply_gate(amplitudes, matrix, factors, target):

    def on_low(values):
        mixed_rows = jnp.einsum("bhmk,ik->bhmi", values, matrix, precision=lax.Precision.HIGHEST)
        return mixed_rows * factors[:, None, None, :]

    def on_high(values):
        mixed_rows = jnp.einsum("bjmk,ij->bimk", values, matrix, precision=lax.Precision.HIGHEST)
        return mixed_rows * factors[:, :, None, None]

    return lax.cond(target == 0, on_low, on_high, amplitudes)


def square_sums(values):
    return (values, jnp.sum(values * values, axis=(1, 2, 3)))


def body_general(states, gate_blocks, kraus_picks, block_targets):
    traj_here = states.shape[0]
    amp_local = states.shape[1]
    register = gate_blocks.shape[-1]
    blocks = gate_blocks.shape[1]
    middle = amp_local // (register * register)
    total_amps = amp_local * lax.axis_size("amp")
    sections = lax.axis_size("segment")
    amplitudes = states.reshape(traj_here, register, middle, register)
    local_sums = [jnp.sum(amplitudes * amplitudes, axis=(1, 2, 3))]
    for section in range(sections):
        owned = jnp.where(lax.axis_index("segment") == section, gate_blocks, jnp.zeros_like(gate_blocks))
        section_gates = lax.psum(owned, "segment")[0]
        for block_pos in range(blocks):
            factors = noise_factors(kraus_picks[:, section, block_pos, :])
            amplitudes = apply_gate(
                amplitudes, section_gates[block_pos], factors, block_targets[section, block_pos]
            )
        amplitudes, local_sq = square_sums(
            lax.all_to_all(amplitudes, "amp", split_axis=1, concat_axis=1, tiled=True)
        )
        local_sums.append(local_sq)
    totals = lax.psum(jnp.stack(local_sums, axis=1), "amp")
    log_weights = jnp.log(totals[:, 1:] / totals[:, :-1])
    amplitudes = amplitudes / jnp.sqrt(totals[:, -1] / total_amps)[:, None, None, None]
    return (amplitudes.reshape(traj_here, amp_local), log_weights)


def solution(mesh):
    in_specs = (
        P("segment", "amp"),
        P("segment", None, None, None),
        P("segment", None, None, None),
        P(),
    )
    out_specs = (P("segment", "amp"), P("segment", None))
    amp, sections = mesh.shape["amp"], mesh.shape["segment"]

    def run(states, gate_blocks, kraus_picks, block_targets):
        register = gate_blocks.shape[-1]
        middle = states.shape[1] // amp // (register * register)
        power_of_two = amp > 1 and amp & (amp - 1) == 0 and sections & (sections - 1) == 0
        fits = middle > 0 and middle % amp == 0 and register % (8 * amp) == 0
        fast = power_of_two and fits and sections % 2 == 0 and sections < EXTRA and states.shape[0] == sections

        def body(*args):
            return (body_fast if fast else body_general)(*args)

        step = jax.shard_map(body, mesh=mesh, in_specs=in_specs, out_specs=out_specs, check_vma=False)
        return step(states, gate_blocks, kraus_picks, block_targets)

    return run
```

profile of v0, /device:TPU:0, one launch (start us, length us, event | category | flops | bytes accessed | tf_op | source)
XLA Modules:
  0.0 72.1 jit_solution(593249075927258483)
XLA Ops:
  0.6 1.1 %slice.4.x_ref = f32[128,8,128]{2,1,0:T(8,128)S(1)} slice(f32[128,16,128]{2,1,0:T(8,128)} %bitcast.8), slice={[0:128], [8:16], [0:128]} | slice | bytes 1048576 | tf_op jit(solution)/shard_map/slice | solution.py:248
  2.3 1.2 %shard_map.59 = (f32[2,128,128]{2,1,0:T(8,128)S(1)}, f32[2,128,128]{2,1,0:T(8,128)S(1)}, f32[2,128,128]{2,1,0:T(8,128)S(1)}, f32[2,128,128]{2,1,0:T(8,128)S(1)}) custom-call(f32[128,16,128]{2,1,0:T(8,128)} %bitcast.9), custom_call_target="tpu_custom_call" | custom-call | tf_op jit(solution)/shard_map/pallas_call | solution.py:223
  3.5 2.7 %collective-permute-start = (f32[2,128,128]{2,1,0:T(8,128)S(1)}, f32[2,128,128]{2,1,0:T(8,128)S(1)}, u32[]{:S(2)}, u32[]{:S(2)}) collective-permute-start(f32[2,128,128]{2,1,0:T(8,128)S(1)} %get-tuple-element.30), channel_id=1, source_target_pairs={{0,2},{1,3},{2,0},{3,1},{4,6},{5,7},{6,4},{7,5},{8,10},{9,11},{10,... | collective-permute-start | bytes 393224 | tf_op jit(solution)/shard_map/ppermute | solution.py:205
  6.1 2.6 %collective-permute-start.1 = (f32[2,128,128]{2,1,0:T(8,128)S(1)}, f32[2,128,128]{2,1,0:T(8,128)S(1)}, u32[]{:S(2)}, u32[]{:S(2)}) collective-permute-start(f32[2,128,128]{2,1,0:T(8,128)S(1)} %get-tuple-element.31), channel_id=1, source_target_pairs={{0,4},{1,5},{2,6},{3,7},{4,0},{5,1},{6,2},{7,3},{8,12},{9,13},{10,... | collective-permute-start | bytes 393224 | tf_op jit(solution)/shard_map/ppermute | solution.py:205
  8.7 2.7 %collective-permute-start.6 = (f32[3,128,128]{2,1,0:T(8,128)S(1)}, f32[3,128,128]{2,1,0:T(8,128)S(1)}, u32[]{:S(2)}, u32[]{:S(2)}) collective-permute-start(f32[3,128,128]{2,1,0:T(8,128)S(1)} %bitcast.4), channel_id=1, source_target_pairs={{0,24},{8,16},{16,8},{24,0},{1,25},{9,17},{17,9},{25,1},{2,26},{10... | collective-permute-start | bytes 589832 | tf_op jit(solution)/shard_map/ppermute | solution.py:205
  12.4 1.7 %collective-permute-start.5 = (f32[3,128,128]{2,1,0:T(8,128)S(1)}, f32[3,128,128]{2,1,0:T(8,128)S(1)}, u32[]{:S(2)}, u32[]{:S(2)}) collective-permute-start(f32[3,128,128]{2,1,0:T(8,128)S(1)} %bitcast.5), channel_id=1, source_target_pairs={{0,16},{8,24},{16,0},{24,8},{1,17},{9,25},{17,1},{25,9},{2,18},{10... | collective-permute-start | bytes 589832 | tf_op jit(solution)/shard_map/ppermute | solution.py:205
  14.2 4.9 %collective-permute-done.1.refs_2_ = f32[2,128,128]{2,1,0:T(8,128)S(1)} collective-permute-done((f32[2,128,128]{2,1,0:T(8,128)S(1)}, f32[2,128,128]{2,1,0:T(8,128)S(1)}, u32[]{:S(2)}, u32[]{:S(2)}) %collective-permute-start.1) | collective-permute-done | bytes 131104 | tf_op jit(solution)/shard_map/ppermute | solution.py:205
  19.2 1.6 %collective-permute-start.4 = (f32[3,128,128]{2,1,0:T(8,128)S(1)}, f32[3,128,128]{2,1,0:T(8,128)S(1)}, u32[]{:S(2)}, u32[]{:S(2)}) collective-permute-start(f32[3,128,128]{2,1,0:T(8,128)S(1)} %bitcast.6), channel_id=1, source_target_pairs={{0,8},{8,0},{16,24},{24,16},{1,9},{9,1},{17,25},{25,17},{2,10},{10... | collective-permute-start | bytes 589832 | tf_op jit(solution)/shard_map/ppermute | solution.py:205
  20.9 2.6 %collective-permute-start.12 = (f32[2,128,128]{2,1,0:T(8,128)S(1)}, f32[2,128,128]{2,1,0:T(8,128)S(1)}, u32[]{:S(2)}, u32[]{:S(2)}) collective-permute-start(f32[2,128,128]{2,1,0:T(8,128)S(1)} %get-tuple-element.44), channel_id=1, source_target_pairs={{0,2},{1,3},{2,0},{3,1},{4,6},{5,7},{6,4},{7,5},{8,10},{9,11},{10,... | collective-permute-start | bytes 393224 | tf_op jit(solution)/shard_map/ppermute | solution.py:205
  23.6 1.1 %collective-permute-start.13 = (f32[2,128,128]{2,1,0:T(8,128)S(1)}, f32[2,128,128]{2,1,0:T(8,128)S(1)}, u32[]{:S(2)}, u32[]{:S(2)}) collective-permute-start(f32[2,128,128]{2,1,0:T(8,128)S(1)} %get-tuple-element.45), channel_id=1, source_target_pairs={{0,4},{1,5},{2,6},{3,7},{4,0},{5,1},{6,2},{7,3},{8,12},{9,13},{10,... | collective-permute-start | bytes 393224 | tf_op jit(solution)/shard_map/ppermute | solution.py:205
  24.7 1.4 %collective-permute-start.14 = (f32[2,128,128]{2,1,0:T(8,128)S(1)}, f32[2,128,128]{2,1,0:T(8,128)S(1)}, u32[]{:S(2)}, u32[]{:S(2)}) collective-permute-start(f32[2,128,128]{2,1,0:T(8,128)S(1)} %get-tuple-element.46), channel_id=1, source_target_pairs={{0,6},{1,7},{2,4},{3,5},{4,2},{5,3},{6,0},{7,1},{8,14},{9,15},{10,... | collective-permute-start | bytes 393224 | tf_op jit(solution)/shard_map/ppermute | solution.py:205
  26.8 2.0 %shard_map.61 = (bf16[4,256,256]{2,1,0:T(8,128)(2,1)S(1)}, bf16[4,256,256]{2,1,0:T(8,128)(2,1)S(1)}) custom-call(s32[4,3,7]{2,1,0:T(4,128)S(1)} %copy.6.picks_ref, s32[4,3]{1,0:T(4,128)S(1)} %copy-done.1, f32[3,128,128]{2,1,0:T(8,128)S(1)} %bitcast.7, f32[3,128,128]{2,1,0:T(8,128)S(1)} %collective-permute-done.4.refs_1_, ...), custom_call_target="tpu_custom_call" | custom-call | tf_op jit(solution)/shard_map/pallas_call | solution.py:223
  28.8 2.3 %shard_map.62 = (f32[2,128,128]{2,1,0:T(8,128)S(1)}, f32[2,128,128]{2,1,0:T(8,128)S(1)}, f32[2,128,128]{2,1,0:T(8,128)S(1)}, f32[2,128,128]{2,1,0:T(8,128)S(1)}, f32[8,128]{1,0:T(8,128)S(1)}) custom-call(f32[4,128,128]{2,1,0:T(8,128)S(1)} %get-tuple-element.33.refs_0_, f32[4,128,128]{2,1,0:T(8,128)S(1)} %collective-permute-done.3.refs_1_, ...), custom_call_target="tpu_custom_call" | custom-call | tf_op jit(solution)/shard_map/pallas_call | solution.py:223
  31.2 5.3 %collective-permute-done.13.refs_2_ = f32[2,128,128]{2,1,0:T(8,128)S(1)} collective-permute-done((f32[2,128,128]{2,1,0:T(8,128)S(1)}, f32[2,128,128]{2,1,0:T(8,128)S(1)}, u32[]{:S(2)}, u32[]{:S(2)}) %collective-permute-start.13) | collective-permute-done | bytes 131104 | tf_op jit(solution)/shard_map/ppermute | solution.py:205
  36.4 2.3 %shard_map.65 = (f32[4,136,128]{2,1,0:T(8,128)S(1)}, f32[4,136,128]{2,1,0:T(8,128)S(1)}) custom-call(f32[2,128,128]{2,1,0:T(8,128)S(1)} %get-tuple-element.43.refs_0_, f32[2,128,128]{2,1,0:T(8,128)S(1)} %collective-permute-done.12.refs_1_, f32[2,128,128]{2,1,0:T(8,128)S(1)} %collective-permute-done.13.refs_2_, ...), custom_call_target="tpu_custom_call" | custom-call | tf_op jit(solution)/shard_map/pallas_call | solution.py:223
  38.9 2.4 %collective-permute-start.7 = (f32[2,128,128]{2,1,0:T(8,128)S(1)}, f32[2,128,128]{2,1,0:T(8,128)S(1)}, u32[]{:S(2)}, u32[]{:S(2)}) collective-permute-start(f32[2,128,128]{2,1,0:T(8,128)S(1)} %get-tuple-element.38), channel_id=1, source_target_pairs={{0,2},{1,3},{2,0},{3,1},{4,6},{5,7},{6,4},{7,5},{8,10},{9,11},{10,... | collective-permute-start | bytes 393224 | tf_op jit(solution)/shard_map/ppermute | solution.py:205
  42.3 1.4 %collective-permute-start.9 = (f32[2,128,128]{2,1,0:T(8,128)S(1)}, f32[2,128,128]{2,1,0:T(8,128)S(1)}, u32[]{:S(2)}, u32[]{:S(2)}) collective-permute-start(f32[2,128,128]{2,1,0:T(8,128)S(1)} %get-tuple-element.40), channel_id=1, source_target_pairs={{0,6},{1,7},{2,4},{3,5},{4,2},{5,3},{6,0},{7,1},{8,14},{9,15},{10,... | collective-permute-start | bytes 393224 | tf_op jit(solution)/shard_map/ppermute | solution.py:205
  43.7 3.8 %collective-permute-done.7.refs_1_ = f32[2,128,128]{2,1,0:T(8,128)S(1)} collective-permute-done((f32[2,128,128]{2,1,0:T(8,128)S(1)}, f32[2,128,128]{2,1,0:T(8,128)S(1)}, u32[]{:S(2)}, u32[]{:S(2)}) %collective-permute-start.7) | collective-permute-done | bytes 131104 | tf_op jit(solution)/shard_map/ppermute | solution.py:205
  47.5 6.7 %collective-permute-done.8.refs_2_ = f32[2,128,128]{2,1,0:T(8,128)S(1)} collective-permute-done((f32[2,128,128]{2,1,0:T(8,128)S(1)}, f32[2,128,128]{2,1,0:T(8,128)S(1)}, u32[]{:S(2)}, u32[]{:S(2)}) %collective-permute-start.8) | collective-permute-done | bytes 131104 | tf_op jit(solution)/shard_map/ppermute | solution.py:205
  54.4 2.6 %collective-permute-start.16 = (f32[2,136,128]{2,1,0:T(8,128)S(1)}, f32[2,136,128]{2,1,0:T(8,128)S(1)}, u32[]{:S(2)}, u32[]{:S(2)}) collective-permute-start(f32[2,136,128]{2,1,0:T(8,128)S(1)} %get-tuple-element.51), channel_id=1, source_target_pairs={{0,2},{1,3},{2,0},{3,1},{4,6},{5,7},{6,4},{7,5},{8,10},{9,11},{10,... | collective-permute-start | bytes 417800 | tf_op jit(solution)/shard_map/ppermute | solution.py:205
  58.0 1.4 %collective-permute-start.18 = (f32[2,136,128]{2,1,0:T(8,128)S(1)}, f32[2,136,128]{2,1,0:T(8,128)S(1)}, u32[]{:S(2)}, u32[]{:S(2)}) collective-permute-start(f32[2,136,128]{2,1,0:T(8,128)S(1)} %get-tuple-element.53), channel_id=1, source_target_pairs={{0,6},{1,7},{2,4},{3,5},{4,2},{5,3},{6,0},{7,1},{8,14},{9,15},{10,... | collective-permute-start | bytes 417800 | tf_op jit(solution)/shard_map/ppermute | solution.py:205
  59.4 4.3 %collective-permute-done.16.refs_3_ = f32[2,136,128]{2,1,0:T(8,128)S(1)} collective-permute-done((f32[2,136,128]{2,1,0:T(8,128)S(1)}, f32[2,136,128]{2,1,0:T(8,128)S(1)}, u32[]{:S(2)}, u32[]{:S(2)}) %collective-permute-start.16) | collective-permute-done | bytes 139296 | tf_op jit(solution)/shard_map/ppermute | solution.py:205
  63.7 6.7 %collective-permute-done.17.refs_4_ = f32[2,136,128]{2,1,0:T(8,128)S(1)} collective-permute-done((f32[2,136,128]{2,1,0:T(8,128)S(1)}, f32[2,136,128]{2,1,0:T(8,128)S(1)}, u32[]{:S(2)}, u32[]{:S(2)}) %collective-permute-start.17) | collective-permute-done | bytes 139296 | tf_op jit(solution)/shard_map/ppermute | solution.py:205
  70.4 1.6 %shard_map.67 = (f32[128,16,128]{2,1,0:T(8,128)}, f32[1,4]{1,0:T(1,128)}) custom-call(f32[4,128,128]{2,1,0:T(8,128)S(1)} %get-tuple-element.41.refs_0_, f32[4,128,128]{2,1,0:T(8,128)S(1)} %collective-permute-done.10.refs_1_, f32[2,136,128]{2,1,0:T(8,128)S(1)} %get-tuple-element.50.refs_2_, f32[2,136,128]{2,1,0:T(8,128)S(1)} %collective-permute-done.16.refs_3_, ...), custom_call_target="tpu_custom_call" | custom-call | tf_op jit(solution)/shard_map/pallas_call | solution.py:223
  (31 shorter events, 4.9 us)
Async XLA Ops:
  1.7 7.0 %copy-start = (f32[1,3,128,128]{3,2,1,0:T(8,128)S(1)}, f32[1,3,128,128]{3,2,1,0:T(8,128)}, u32[]{:S(2)}) copy-start(f32[1,3,128,128]{3,2,1,0:T(8,128)} %param.5) | copy-start | bytes 589828
  1.7 19.0 %collective-permute-start.11 = (f32[128,8,128]{2,1,0:T(8,128)S(1)}, f32[128,8,128]{2,1,0:T(8,128)S(1)}, u32[]{:S(2)}, u32[]{:S(2)}) collective-permute-start(f32[128,8,128]{2,1,0:T(8,128)S(1)} %slice.4.x_ref), channel_id=1, source_target_pairs={{0,1},{1,0},{2,3},{3,2},{4,5},{5,4},{6,7},{7,6},{8,9},{9,8},{10,11... | collective-permute-start | bytes 1572872 | tf_op jit(solution)/shard_map/ppermute | solution.py:205
  3.5 9.0 %collective-permute-start = (f32[2,128,128]{2,1,0:T(8,128)S(1)}, f32[2,128,128]{2,1,0:T(8,128)S(1)}, u32[]{:S(2)}, u32[]{:S(2)}) collective-permute-start(f32[2,128,128]{2,1,0:T(8,128)S(1)} %get-tuple-element.30), channel_id=1, source_target_pairs={{0,2},{1,3},{2,0},{3,1},{4,6},{5,7},{6,4},{7,5},{8,10},{9,11},{10,... | collective-permute-start | bytes 393224 | tf_op jit(solution)/shard_map/ppermute | solution.py:205
  6.1 12.9 %collective-permute-start.1 = (f32[2,128,128]{2,1,0:T(8,128)S(1)}, f32[2,128,128]{2,1,0:T(8,128)S(1)}, u32[]{:S(2)}, u32[]{:S(2)}) collective-permute-start(f32[2,128,128]{2,1,0:T(8,128)S(1)} %get-tuple-element.31), channel_id=1, source_target_pairs={{0,4},{1,5},{2,6},{3,7},{4,0},{5,1},{6,2},{7,3},{8,12},{9,13},{10,... | collective-permute-start | bytes 393224 | tf_op jit(solution)/shard_map/ppermute | solution.py:205
  8.7 10.3 %collective-permute-start.2 = (f32[2,128,128]{2,1,0:T(8,128)S(1)}, f32[2,128,128]{2,1,0:T(8,128)S(1)}, u32[]{:S(2)}, u32[]{:S(2)}) collective-permute-start(f32[2,128,128]{2,1,0:T(8,128)S(1)} %get-tuple-element.32), channel_id=1, source_target_pairs={{0,6},{1,7},{2,4},{3,5},{4,2},{5,3},{6,0},{7,1},{8,14},{9,15},{10,... | collective-permute-start | bytes 393224 | tf_op jit(solution)/shard_map/ppermute | solution.py:205
  8.7 14.8 %collective-permute-start.6 = (f32[3,128,128]{2,1,0:T(8,128)S(1)}, f32[3,128,128]{2,1,0:T(8,128)S(1)}, u32[]{:S(2)}, u32[]{:S(2)}) collective-permute-start(f32[3,128,128]{2,1,0:T(8,128)S(1)} %bitcast.4), channel_id=1, source_target_pairs={{0,24},{8,16},{16,8},{24,0},{1,25},{9,17},{17,9},{25,1},{2,26},{10... | collective-permute-start | bytes 589832 | tf_op jit(solution)/shard_map/ppermute | solution.py:205
  12.4 12.2 %collective-permute-start.5 = (f32[3,128,128]{2,1,0:T(8,128)S(1)}, f32[3,128,128]{2,1,0:T(8,128)S(1)}, u32[]{:S(2)}, u32[]{:S(2)}) collective-permute-start(f32[3,128,128]{2,1,0:T(8,128)S(1)} %bitcast.5), channel_id=1, source_target_pairs={{0,16},{8,24},{16,0},{24,8},{1,17},{9,25},{17,1},{25,9},{2,18},{10... | collective-permute-start | bytes 589832 | tf_op jit(solution)/shard_map/ppermute | solution.py:205
  19.1 9.7 %collective-permute-start.3 = (f32[4,128,128]{2,1,0:T(8,128)S(1)}, f32[4,128,128]{2,1,0:T(8,128)S(1)}, u32[]{:S(2)}, u32[]{:S(2)}) collective-permute-start(f32[4,128,128]{2,1,0:T(8,128)S(1)} %get-tuple-element.34), channel_id=1, source_target_pairs={{0,1},{1,0},{2,3},{3,2},{4,5},{5,4},{6,7},{7,6},{8,9},{9,8},{10,11... | collective-permute-start | bytes 786440 | tf_op jit(solution)/shard_map/ppermute | solution.py:205
  19.2 7.3 %collective-permute-start.4 = (f32[3,128,128]{2,1,0:T(8,128)S(1)}, f32[3,128,128]{2,1,0:T(8,128)S(1)}, u32[]{:S(2)}, u32[]{:S(2)}) collective-permute-start(f32[3,128,128]{2,1,0:T(8,128)S(1)} %bitcast.6), channel_id=1, source_target_pairs={{0,8},{8,0},{16,24},{24,16},{1,9},{9,1},{17,25},{25,17},{2,10},{10... | collective-permute-start | bytes 589832 | tf_op jit(solution)/shard_map/ppermute | solution.py:205
  20.9 5.2 %copy-start.2 = (s32[1,4,3,7]{3,1,2,0:T(4,128)S(1)}, s32[1,4,3,7]{3,1,2,0:T(4,128)}, u32[]{:S(2)}) copy-start(s32[1,4,3,7]{3,1,2,0:T(4,128)} %param.6) | copy-start | bytes 1012
  20.9 10.3 %collective-permute-start.12 = (f32[2,128,128]{2,1,0:T(8,128)S(1)}, f32[2,128,128]{2,1,0:T(8,128)S(1)}, u32[]{:S(2)}, u32[]{:S(2)}) collective-permute-start(f32[2,128,128]{2,1,0:T(8,128)S(1)} %get-tuple-element.44), channel_id=1, source_target_pairs={{0,2},{1,3},{2,0},{3,1},{4,6},{5,7},{6,4},{7,5},{8,10},{9,11},{10,... | collective-permute-start | bytes 393224 | tf_op jit(solution)/shard_map/ppermute | solution.py:205
  23.6 12.9 %collective-permute-start.13 = (f32[2,128,128]{2,1,0:T(8,128)S(1)}, f32[2,128,128]{2,1,0:T(8,128)S(1)}, u32[]{:S(2)}, u32[]{:S(2)}) collective-permute-start(f32[2,128,128]{2,1,0:T(8,128)S(1)} %get-tuple-element.45), channel_id=1, source_target_pairs={{0,4},{1,5},{2,6},{3,7},{4,0},{5,1},{6,2},{7,3},{8,12},{9,13},{10,... | collective-permute-start | bytes 393224 | tf_op jit(solution)/shard_map/ppermute | solution.py:205
  24.7 11.8 %collective-permute-start.14 = (f32[2,128,128]{2,1,0:T(8,128)S(1)}, f32[2,128,128]{2,1,0:T(8,128)S(1)}, u32[]{:S(2)}, u32[]{:S(2)}) collective-permute-start(f32[2,128,128]{2,1,0:T(8,128)S(1)} %get-tuple-element.46), channel_id=1, source_target_pairs={{0,6},{1,7},{2,4},{3,5},{4,2},{5,3},{6,0},{7,1},{8,14},{9,15},{10,... | collective-permute-start | bytes 393224 | tf_op jit(solution)/shard_map/ppermute | solution.py:205
  26.1 0.7 copy-start.1
  38.8 15.5 %collective-permute-start.15 = (f32[4,136,128]{2,1,0:T(8,128)S(1)}, f32[4,136,128]{2,1,0:T(8,128)S(1)}, u32[]{:S(2)}, u32[]{:S(2)}) collective-permute-start(f32[4,136,128]{2,1,0:T(8,128)S(1)} %get-tuple-element.49), channel_id=1, source_target_pairs={{0,1},{1,0},{2,3},{3,2},{4,5},{5,4},{6,7},{7,6},{8,9},{9,8},{10,11... | collective-permute-start | bytes 835592 | tf_op jit(solution)/shard_map/ppermute | solution.py:205
  38.9 8.6 %collective-permute-start.7 = (f32[2,128,128]{2,1,0:T(8,128)S(1)}, f32[2,128,128]{2,1,0:T(8,128)S(1)}, u32[]{:S(2)}, u32[]{:S(2)}) collective-permute-start(f32[2,128,128]{2,1,0:T(8,128)S(1)} %get-tuple-element.38), channel_id=1, source_target_pairs={{0,2},{1,3},{2,0},{3,1},{4,6},{5,7},{6,4},{7,5},{8,10},{9,11},{10,... | collective-permute-start | bytes 393224 | tf_op jit(solution)/shard_map/ppermute | solution.py:205
  41.3 12.9 %collective-permute-start.8 = (f32[2,128,128]{2,1,0:T(8,128)S(1)}, f32[2,128,128]{2,1,0:T(8,128)S(1)}, u32[]{:S(2)}, u32[]{:S(2)}) collective-permute-start(f32[2,128,128]{2,1,0:T(8,128)S(1)} %get-tuple-element.39), channel_id=1, source_target_pairs={{0,4},{1,5},{2,6},{3,7},{4,0},{5,1},{6,2},{7,3},{8,12},{9,13},{10,... | collective-permute-start | bytes 393224 | tf_op jit(solution)/shard_map/ppermute | solution.py:205
  42.3 11.9 %collective-permute-start.9 = (f32[2,128,128]{2,1,0:T(8,128)S(1)}, f32[2,128,128]{2,1,0:T(8,128)S(1)}, u32[]{:S(2)}, u32[]{:S(2)}) collective-permute-start(f32[2,128,128]{2,1,0:T(8,128)S(1)} %get-tuple-element.40), channel_id=1, source_target_pairs={{0,6},{1,7},{2,4},{3,5},{4,2},{5,3},{6,0},{7,1},{8,14},{9,15},{10,... | collective-permute-start | bytes 393224 | tf_op jit(solution)/shard_map/ppermute | solution.py:205
  54.2 5.2 %collective-permute-start.10 = (f32[4,128,128]{2,1,0:T(8,128)S(1)}, f32[4,128,128]{2,1,0:T(8,128)S(1)}, u32[]{:S(2)}, u32[]{:S(2)}) collective-permute-start(f32[4,128,128]{2,1,0:T(8,128)S(1)} %get-tuple-element.42), channel_id=1, source_target_pairs={{0,1},{1,0},{2,3},{3,2},{4,5},{5,4},{6,7},{7,6},{8,9},{9,8},{10,11... | collective-permute-start | bytes 786440 | tf_op jit(solution)/shard_map/ppermute | solution.py:205
  54.4 9.4 %collective-permute-start.16 = (f32[2,136,128]{2,1,0:T(8,128)S(1)}, f32[2,136,128]{2,1,0:T(8,128)S(1)}, u32[]{:S(2)}, u32[]{:S(2)}) collective-permute-start(f32[2,136,128]{2,1,0:T(8,128)S(1)} %get-tuple-element.51), channel_id=1, source_target_pairs={{0,2},{1,3},{2,0},{3,1},{4,6},{5,7},{6,4},{7,5},{8,10},{9,11},{10,... | collective-permute-start | bytes 417800 | tf_op jit(solution)/shard_map/ppermute | solution.py:205
  57.0 13.5 %collective-permute-start.17 = (f32[2,136,128]{2,1,0:T(8,128)S(1)}, f32[2,136,128]{2,1,0:T(8,128)S(1)}, u32[]{:S(2)}, u32[]{:S(2)}) collective-permute-start(f32[2,136,128]{2,1,0:T(8,128)S(1)} %get-tuple-element.52), channel_id=1, source_target_pairs={{0,4},{1,5},{2,6},{3,7},{4,0},{5,1},{6,2},{7,3},{8,12},{9,13},{10,... | collective-permute-start | bytes 417800 | tf_op jit(solution)/shard_map/ppermute | solution.py:205
  58.0 12.4 %collective-permute-start.18 = (f32[2,136,128]{2,1,0:T(8,128)S(1)}, f32[2,136,128]{2,1,0:T(8,128)S(1)}, u32[]{:S(2)}, u32[]{:S(2)}) collective-permute-start(f32[2,136,128]{2,1,0:T(8,128)S(1)} %get-tuple-element.53), channel_id=1, source_target_pairs={{0,6},{1,7},{2,4},{3,5},{4,2},{5,3},{6,0},{7,1},{8,14},{9,15},{10,... | collective-permute-start | bytes 417800 | tf_op jit(solution)/shard_map/ppermute | solution.py:205
where the time goes:
time: 72.3 us; the launch traced here: 72.1 us
  waiting for transfers between devices  33.1 us (46%)
  starting transfers between devices  27.1 us (37%)
  Pallas kernels  9.72 us (13%)
  local copies, waits for them, and re-layouts  1.39 us (2%)
  between operations  0.76 us (1%)
    ppermute x19, waiting for transfers between devices, swap(): return lax.ppermute(piece, axis, [(i, i ^ k) for i in range(size)])  33.1 us
    ppermute x19, starting transfers between devices, swap(): return lax.ppermute(piece, axis, [(i, i ^ k) for i in range(size)])  27.1 us
    pallas_call x9, Pallas kernels, kernel(): pl.pallas_call(body, out_shape=out_shape, compiler_params=params, **specs...  9.72 us
  transfers between devices with their start and end apart: 19, of which 8 were waited for; matrix products, arithmetic and copies ran while one was open for 0% of the time, Pallas kernels for 8%

commit v1 on v0

--- a/solution.py
+++ b/solution.py
@@ -15,6 +15,7 @@
 VMEM = pl.BlockSpec(memory_space=pltpu.VMEM)
 SMEM = pl.BlockSpec(memory_space=pltpu.SMEM)
 EXTRA = 8
+STEPS = 4
 VMEM_LIMIT = 12 * 2**20
 
 
@@ -23,13 +24,23 @@
     return high, (value - high.astype(F32)).astype(BF16)
 
 
-def pack_kernel(x_ref, *out_refs):
+def pack_kernel(steps, x_ref, *refs):
     me = lax.axis_index("amp")
-    register, middle, lanes = x_ref.shape
-    rows = x_ref.reshape(register * middle, lanes)
-    for far, out in enumerate(out_refs):
-        for near in range(2):
-            out[near] = rows[pl.ds(me ^ (2 * far + near), register, stride=middle), :]
+    out_refs, held, sems = refs[:-2], refs[-2], refs[-1]
+    register, middle, lanes = held.shape
+    step = register // steps
+    copies = []
+    for at in range(steps):
+        span = pl.ds(at * step, step)
+        copies.append(pltpu.make_async_copy(x_ref.at[span, 0:middle, :], held.at[span], sems.at[at]))
+        copies[-1].start()
+    rows = held.reshape(register * middle, lanes)
+    for at in range(steps):
+        copies[at].wait()
+        for far, out in enumerate(out_refs):
+            for near in range(2):
+                first = at * step * middle + (me ^ (2 * far + near))
+                out[near, at * step : (at + 1) * step, :] = rows[pl.ds(first, step, stride=middle), :]
 
 
 def pack_both_kernel(x_ref, side_ref, *out_refs):
@@ -48,10 +59,22 @@
         refs[lines + 1][far] = refs[far][1]
 
 
+def part_last_kernel(piece_ref, near_ref, other_ref):
+    register = near_ref.shape[1]
+    sums = piece_ref[2 * register :, :]
+    for near, out in enumerate((near_ref, other_ref)):
+        out[:register, :] = piece_ref[near * register : (near + 1) * register, :]
+        out[register:, :] = sums
+
+
 def join_kernel(own_ref, other_ref, *out_refs):
+    register = own_ref.shape[1]
+    last = len(out_refs) * register
+    sums = own_ref[last:, :] + other_ref[last:, :]
     for far, out in enumerate(out_refs):
-        out[0] = own_ref[far]
-        out[1] = other_ref[far]
+        for near, ref in enumerate((own_ref, other_ref)):
+            out[near * register : (near + 1) * register, :] = ref[far * register : (far + 1) * register, :]
+        out[2 * register :, :] = sums
 
 
 def pick_of(pick, factors):
@@ -160,43 +183,58 @@
                     x[:, part * rest : (part + 1) * rest, :] = piece.reshape(amp, rest, lanes)
         sums.append(total)
     rows = jnp.concatenate(sums + [jnp.zeros((EXTRA - len(sums), lanes), F32)], axis=0)
-    if last:
-        rows = rows + sums_in[...]
-    else:
+    if not last:
+        for far in range(lines):
+            for near in range(2):
+                out_refs[far][near] = x[me ^ (2 * far + near)]
         out_refs[lines][...] = rows
-    for far in range(lines):
-        for near in range(2):
-            out = piece_of(out_refs if last else out_refs[:lines], far, near)
-            out[0:register, :] = x[me ^ (2 * far + near)]
-            if last:
-                out[register:, :] = rows
-
-
-def unpack_kernel(lines, counts, total_amps, *refs):
-    held = []
-    for count in counts:
-        held, refs = held + [refs[:count]], refs[count:]
-    x_ref, logs_ref = refs
+        return
+    rows = rows + sums_in[...]
+    first = out_refs[0]
+    for near in range(2):
+        first[near * register : (near + 1) * register, :] = x[me ^ (2 * (lines - 1) + near)]
+        for far in range(lines - 1):
+            out_refs[1 + near][far * register : (far + 1) * register, :] = x[me ^ (2 * far + near)]
+        out_refs[1 + near][(lines - 1) * register :, :] = rows
+    first[2 * register :, :] = rows
+
+
+def unpack_kernel(lines, early, steps, total_amps, *refs):
+    held, refs = refs[: 2 * early], refs[2 * early :]
+    joined, far_refs, (x_ref, logs_ref, out, sems) = refs[: lines - 1], refs[lines - 1 : lines + 1], refs[lines + 1 :]
     me = lax.axis_index("amp")
-    register, middle, lanes = x_ref.shape
+    register, middle, lanes = out.shape
     sections = logs_ref.shape[1]
-    totals = jnp.zeros((EXTRA, lanes), F32)
-    for far in range(lines):
-        for near in range(2):
-            totals = totals + piece_of(held[-1], far, near)[register:, :]
+    totals = far_refs[0][register:, :] + far_refs[1][register:, :]
+    for ref in joined:
+        totals = totals + ref[2 * register :, :]
     totals = jnp.sum(totals, axis=1, keepdims=True)
+    scale = 1.0 / jnp.sqrt(totals[sections : sections + 1] / total_amps)
+    flat = out.reshape(register * middle, lanes)
+    step = register // steps
+    copies = []
+    for at in range(steps):
+        low, high = at * step, (at + 1) * step
+        for chunk in range(early + 1):
+            for far in range(lines):
+                for near in range(2):
+                    if chunk < early:
+                        value = held[2 * chunk + near][far, low:high, :]
+                    elif far < lines - 1:
+                        value = joined[far][near * register + low : near * register + high, :]
+                    else:
+                        value = far_refs[near][low:high, :]
+                    m = chunk * 2 * lines + (me ^ (2 * far + near))
+                    flat[pl.ds(low * middle + m, step, stride=middle), :] = value * scale
+        span = pl.ds(low, step)
+        copies.append(pltpu.make_async_copy(out.at[span], x_ref.at[span], sems.at[at]))
+        copies[-1].start()
     logs = jnp.log(totals[1 : sections + 1] / totals[:sections])
     rows = lax.broadcasted_iota(jnp.int32, (sections, sections), 0)
     columns = lax.broadcasted_iota(jnp.int32, (sections, sections), 1)
     logs_ref[...] = jnp.sum(jnp.where(rows == columns, logs, 0.0), axis=0, keepdims=True)
-    scale = 1.0 / jnp.sqrt(totals[sections : sections + 1] / total_amps)
-    out = x_ref.reshape(register * middle, lanes)
-    for chunk, pieces in enumerate(held):
-        for far in range(lines):
-            for near in range(2):
-                value = piece_of(pieces, far, near)[0:register, :]
-                m = chunk * 2 * lines + (me ^ (2 * far + near))
-                out[pl.ds(m, register, stride=middle), :] = value * scale
+    for copy in copies:
+        copy.wait()
 
 
 def swap(piece, k, size, axis):
@@ -216,15 +254,14 @@
     def array(*shape, dtype=F32):
         return jax.ShapeDtypeStruct(shape, dtype)
 
-    def kernel(body, out_shape, *operands, in_specs=None, **options):
-        specs = dict(in_specs=in_specs or [VMEM] * len(operands))
-        if "grid" not in options:
-            specs["out_specs"] = [VMEM] * len(out_shape)
-        return pl.pallas_call(body, out_shape=out_shape, compiler_params=params, **specs, **options)(*operands)
+    def kernel(body, out_shape, *operands, **options):
+        specs = dict(in_specs=[VMEM] * len(operands), out_specs=[VMEM] * len(out_shape))
+        return pl.pallas_call(body, out_shape=out_shape, compiler_params=params, **{**specs, **options})(*operands)
 
     def along(pieces):
-        back = {far: swap(pieces[far], 2 * far, amp, "amp") for far in range(lines - 1, -1, -1)}
-        return [back[far] for far in range(lines)]
+        count = len(pieces)
+        back = {far: swap(pieces[far], 2 * far, amp, "amp") for far in range(count - 1, -1, -1)}
+        return [back[far] for far in range(count)]
 
     def across(piece):
         return swap(piece, 1, amp, "amp")
@@ -235,12 +272,11 @@
     for chunk in range(chunks):
         if chunk == 0:
             packed = kernel(
-                pack_kernel,
+                functools.partial(pack_kernel, STEPS),
                 pairs,
                 pltpu.with_memory_space_constraint(x, pltpu.HBM),
-                grid=(1,),
-                in_specs=[pl.BlockSpec((register, amp, register), lambda i: (0, 0, 0))],
-                out_specs=[pl.BlockSpec((2, register, register), lambda i: (0, 0, 0))] * lines,
+                in_specs=[pl.BlockSpec(memory_space=pltpu.HBM)],
+                scratch_shapes=[pltpu.VMEM((register, amp, register), F32), pltpu.SemaphoreType.DMA((STEPS,))],
             )
             near, other = kernel(part_kernel, halves, *along(packed))
             arrived.append([near, across(other)])
@@ -262,9 +298,11 @@
     carried, held = [], []
     for chunk, pieces in enumerate(arrived):
         last = chunk == chunks - 1
+        both = 2 * register + EXTRA
+        aside = array((lines - 1) * register + EXTRA, register)
         results = kernel(
             functools.partial(sections_kernel, sections, lines, len(pieces), last),
-            [array(lines, register + EXTRA, register)] * 2 if last else pairs + [array(EXTRA, register)],
+            [array(both, register), aside, aside] if last else pairs + [array(EXTRA, register)],
             *pieces,
             low,
             high,
@@ -272,19 +310,24 @@
             scratch_shapes=[pltpu.VMEM((amp, register, register), F32)],
         )
         if last:
-            own, other = results
-            tall = [array(2, register + EXTRA, register)] * lines
-            joined = kernel(join_kernel, tall, own, across(other))
-            held.append(along(joined))
+            first, own, other = results
+            first = swap(first, 2 * (lines - 1), amp, "amp")
+            tall = [array(both, register)] * (lines - 1)
+            held += along(kernel(join_kernel, tall, own, across(other)))
+            tall = [array(register + EXTRA, register)] * 2
+            near, other = kernel(part_last_kernel, tall, first)
+            held += [near, across(other)]
         else:
             carried = [results[lines]]
             near, other = kernel(part_kernel, halves, *along(results[:lines]))
-            held.append([near, across(other)])
+            held += [near, across(other)]
 
     out, logs = kernel(
-        functools.partial(unpack_kernel, lines, [len(pieces) for pieces in held], float(amp_local * amp)),
+        functools.partial(unpack_kernel, lines, chunks - 1, STEPS, float(amp_local * amp)),
         [array(register, middle, register), array(1, sections)],
-        *[piece for pieces in held for piece in pieces],
+        *held,
+        out_specs=[pl.BlockSpec(memory_space=pltpu.HBM), VMEM],
+        scratch_shapes=[pltpu.VMEM((register, middle, register), F32), pltpu.SemaphoreType.DMA((STEPS,))],
     )
     return out.reshape(1, amp_local), logs
 
@@ -365,7 +408,7 @@
     def run(states, gate_blocks, kraus_picks, block_targets):
         register = gate_blocks.shape[-1]
         middle = states.shape[1] // amp // (register * register)
-        power_of_two = amp > 1 and amp & (amp - 1) == 0 and sections & (sections - 1) == 0
+        power_of_two = amp > 2 and amp & (amp - 1) == 0 and sections & (sections - 1) == 0
         fits = middle > 0 and middle % amp == 0 and register % (8 * amp) == 0
         fast = power_of_two and fits and sections % 2 == 0 and sections < EXTRA and states.shape[0] == sections
 

time: 72.3 us -> 66.2 us (0.916)
  waiting for transfers between devices: 33.1 us -> 27.4 us
    ppermute x19 -> x20, waiting for transfers between devices: 33.1 us -> 27.4 us  [swap(): return lax.ppermute(piece, axis, [(i, i ^ k) for i in range(size)])]
    ppermute x19 -> x20, starting transfers between devices: 27.1 us -> 26.6 us  [swap(): return lax.ppermute(piece, axis, [(i, i ^ k) for i in range(size)])]
    pallas_call x9 -> x10, Pallas kernels: 9.72 us -> 9.83 us  [kernel(): pl.pallas_call(body, out_shape=out_shape, compiler_params=params, **{**sp...]
  transfers between devices with their start and end apart: 19 -> 20, of which waited for: 8 -> 10; matrix products, arithmetic and copies ran while one was open for 0% -> 0% of each run, Pallas kernels for 8% -> 12%
where the time goes in v1:
time: 66.2 us; the launch traced here: 66 us
  waiting for transfers between devices  27.4 us (41%)
  starting transfers between devices  26.6 us (40%)
  Pallas kernels  9.83 us (15%)
  local copies, waits for them, and re-layouts  1.39 us (2%)
  between operations  0.77 us (1%)
    ppermute x20, waiting for transfers between devices, swap(): return lax.ppermute(piece, axis, [(i, i ^ k) for i in range(size)])  27.4 us
    ppermute x20, starting transfers between devices, swap(): return lax.ppermute(piece, axis, [(i, i ^ k) for i in range(size)])  26.6 us
    pallas_call x10, Pallas kernels, kernel(): pl.pallas_call(body, out_shape=out_shape, compiler_params=params, **{**sp...  9.83 us
  transfers between devices with their start and end apart: 20, of which 10 were waited for; matrix products, arithmetic and copies ran while one was open for 0% of the time, Pallas kernels for 12%

profile of v1, /device:TPU:0, one launch (start us, length us, event | category | flops | bytes accessed | tf_op | source)
XLA Modules:
  0.0 66.0 jit_solution(7603473110521366832)
XLA Ops:
  0.6 1.1 %slice.4.x_ref = f32[128,8,128]{2,1,0:T(8,128)S(1)} slice(f32[128,16,128]{2,1,0:T(8,128)} %bitcast.8), slice={[0:128], [8:16], [0:128]} | slice | bytes 1048576 | tf_op jit(solution)/shard_map/slice | solution.py:284
  2.3 1.2 %shard_map.59 = (f32[2,128,128]{2,1,0:T(8,128)S(1)}, f32[2,128,128]{2,1,0:T(8,128)S(1)}, f32[2,128,128]{2,1,0:T(8,128)S(1)}, f32[2,128,128]{2,1,0:T(8,128)S(1)}) custom-call(f32[128,16,128]{2,1,0:T(8,128)} %bitcast.9), custom_call_target="tpu_custom_call" | custom-call | tf_op jit(solution)/shard_map/pallas_call | solution.py:259
  3.5 2.7 %collective-permute-start = (f32[2,128,128]{2,1,0:T(8,128)S(1)}, f32[2,128,128]{2,1,0:T(8,128)S(1)}, u32[]{:S(2)}, u32[]{:S(2)}) collective-permute-start(f32[2,128,128]{2,1,0:T(8,128)S(1)} %get-tuple-element.32), channel_id=1, source_target_pairs={{0,2},{1,3},{2,0},{3,1},{4,6},{5,7},{6,4},{7,5},{8,10},{9,11},{10,... | collective-permute-start | bytes 393224 | tf_op jit(solution)/shard_map/ppermute | solution.py:243
  6.1 2.6 %collective-permute-start.1 = (f32[2,128,128]{2,1,0:T(8,128)S(1)}, f32[2,128,128]{2,1,0:T(8,128)S(1)}, u32[]{:S(2)}, u32[]{:S(2)}) collective-permute-start(f32[2,128,128]{2,1,0:T(8,128)S(1)} %get-tuple-element.33), channel_id=1, source_target_pairs={{0,4},{1,5},{2,6},{3,7},{4,0},{5,1},{6,2},{7,3},{8,12},{9,13},{10,... | collective-permute-start | bytes 393224 | tf_op jit(solution)/shard_map/ppermute | solution.py:243
  8.7 2.7 %collective-permute-start.6 = (f32[3,128,128]{2,1,0:T(8,128)S(1)}, f32[3,128,128]{2,1,0:T(8,128)S(1)}, u32[]{:S(2)}, u32[]{:S(2)}) collective-permute-start(f32[3,128,128]{2,1,0:T(8,128)S(1)} %bitcast.4), channel_id=1, source_target_pairs={{0,24},{8,16},{16,8},{24,0},{1,25},{9,17},{17,9},{25,1},{2,26},{10... | collective-permute-start | bytes 589832 | tf_op jit(solution)/shard_map/ppermute | solution.py:243
  12.4 1.7 %collective-permute-start.5 = (f32[3,128,128]{2,1,0:T(8,128)S(1)}, f32[3,128,128]{2,1,0:T(8,128)S(1)}, u32[]{:S(2)}, u32[]{:S(2)}) collective-permute-start(f32[3,128,128]{2,1,0:T(8,128)S(1)} %bitcast.5), channel_id=1, source_target_pairs={{0,16},{8,24},{16,0},{24,8},{1,17},{9,25},{17,1},{25,9},{2,18},{10... | collective-permute-start | bytes 589832 | tf_op jit(solution)/shard_map/ppermute | solution.py:243
  14.2 4.9 %collective-permute-done.1.refs_2_ = f32[2,128,128]{2,1,0:T(8,128)S(1)} collective-permute-done((f32[2,128,128]{2,1,0:T(8,128)S(1)}, f32[2,128,128]{2,1,0:T(8,128)S(1)}, u32[]{:S(2)}, u32[]{:S(2)}) %collective-permute-start.1) | collective-permute-done | bytes 131104 | tf_op jit(solution)/shard_map/ppermute | solution.py:243
  19.2 1.6 %collective-permute-start.4 = (f32[3,128,128]{2,1,0:T(8,128)S(1)}, f32[3,128,128]{2,1,0:T(8,128)S(1)}, u32[]{:S(2)}, u32[]{:S(2)}) collective-permute-start(f32[3,128,128]{2,1,0:T(8,128)S(1)} %bitcast.6), channel_id=1, source_target_pairs={{0,8},{8,0},{16,24},{24,16},{1,9},{9,1},{17,25},{25,17},{2,10},{10... | collective-permute-start | bytes 589832 | tf_op jit(solution)/shard_map/ppermute | solution.py:243
  20.9 2.6 %collective-permute-start.12 = (f32[2,128,128]{2,1,0:T(8,128)S(1)}, f32[2,128,128]{2,1,0:T(8,128)S(1)}, u32[]{:S(2)}, u32[]{:S(2)}) collective-permute-start(f32[2,128,128]{2,1,0:T(8,128)S(1)} %get-tuple-element.46), channel_id=1, source_target_pairs={{0,2},{1,3},{2,0},{3,1},{4,6},{5,7},{6,4},{7,5},{8,10},{9,11},{10,... | collective-permute-start | bytes 393224 | tf_op jit(solution)/shard_map/ppermute | solution.py:243
  23.5 1.1 %collective-permute-start.13 = (f32[2,128,128]{2,1,0:T(8,128)S(1)}, f32[2,128,128]{2,1,0:T(8,128)S(1)}, u32[]{:S(2)}, u32[]{:S(2)}) collective-permute-start(f32[2,128,128]{2,1,0:T(8,128)S(1)} %get-tuple-element.47), channel_id=1, source_target_pairs={{0,4},{1,5},{2,6},{3,7},{4,0},{5,1},{6,2},{7,3},{8,12},{9,13},{10,... | collective-permute-start | bytes 393224 | tf_op jit(solution)/shard_map/ppermute | solution.py:243
  24.6 1.4 %collective-permute-start.14 = (f32[2,128,128]{2,1,0:T(8,128)S(1)}, f32[2,128,128]{2,1,0:T(8,128)S(1)}, u32[]{:S(2)}, u32[]{:S(2)}) collective-permute-start(f32[2,128,128]{2,1,0:T(8,128)S(1)} %get-tuple-element.48), channel_id=1, source_target_pairs={{0,6},{1,7},{2,4},{3,5},{4,2},{5,3},{6,0},{7,1},{8,14},{9,15},{10,... | collective-permute-start | bytes 393224 | tf_op jit(solution)/shard_map/ppermute | solution.py:243
  26.8 2.0 %shard_map.61 = (bf16[4,256,256]{2,1,0:T(8,128)(2,1)S(1)}, bf16[4,256,256]{2,1,0:T(8,128)(2,1)S(1)}) custom-call(s32[4,3,7]{2,1,0:T(4,128)S(1)} %copy.6.picks_ref, s32[4,3]{1,0:T(4,128)S(1)} %copy-done.1, f32[3,128,128]{2,1,0:T(8,128)S(1)} %bitcast.7, f32[3,128,128]{2,1,0:T(8,128)S(1)} %collective-permute-done.4.refs_1_, ...), custom_call_target="tpu_custom_call" | custom-call | tf_op jit(solution)/shard_map/pallas_call | solution.py:259
  28.8 2.3 %shard_map.62 = (f32[2,128,128]{2,1,0:T(8,128)S(1)}, f32[2,128,128]{2,1,0:T(8,128)S(1)}, f32[2,128,128]{2,1,0:T(8,128)S(1)}, f32[2,128,128]{2,1,0:T(8,128)S(1)}, f32[8,128]{1,0:T(8,128)S(1)}) custom-call(f32[4,128,128]{2,1,0:T(8,128)S(1)} %get-tuple-element.35.refs_0_, f32[4,128,128]{2,1,0:T(8,128)S(1)} %collective-permute-done.3.refs_1_, ...), custom_call_target="tpu_custom_call" | custom-call | tf_op jit(solution)/shard_map/pallas_call | solution.py:259
  31.1 2.4 %collective-permute-start.7 = (f32[2,128,128]{2,1,0:T(8,128)S(1)}, f32[2,128,128]{2,1,0:T(8,128)S(1)}, u32[]{:S(2)}, u32[]{:S(2)}) collective-permute-start(f32[2,128,128]{2,1,0:T(8,128)S(1)} %get-tuple-element.40), channel_id=1, source_target_pairs={{0,2},{1,3},{2,0},{3,1},{4,6},{5,7},{6,4},{7,5},{8,10},{9,11},{10,... | collective-permute-start | bytes 393224 | tf_op jit(solution)/shard_map/ppermute | solution.py:243
  33.5 1.1 %collective-permute-start.8 = (f32[2,128,128]{2,1,0:T(8,128)S(1)}, f32[2,128,128]{2,1,0:T(8,128)S(1)}, u32[]{:S(2)}, u32[]{:S(2)}) collective-permute-start(f32[2,128,128]{2,1,0:T(8,128)S(1)} %get-tuple-element.41), channel_id=1, source_target_pairs={{0,4},{1,5},{2,6},{3,7},{4,0},{5,1},{6,2},{7,3},{8,12},{9,13},{10,... | collective-permute-start | bytes 393224 | tf_op jit(solution)/shard_map/ppermute | solution.py:243
  34.6 1.4 %collective-permute-start.9 = (f32[2,128,128]{2,1,0:T(8,128)S(1)}, f32[2,128,128]{2,1,0:T(8,128)S(1)}, u32[]{:S(2)}, u32[]{:S(2)}) collective-permute-start(f32[2,128,128]{2,1,0:T(8,128)S(1)} %get-tuple-element.42), channel_id=1, source_target_pairs={{0,6},{1,7},{2,4},{3,5},{4,2},{5,3},{6,0},{7,1},{8,14},{9,15},{10,... | collective-permute-start | bytes 393224 | tf_op jit(solution)/shard_map/ppermute | solution.py:243
  36.4 2.3 %shard_map.65 = (f32[264,128]{1,0:T(8,128)S(1)}, f32[392,128]{1,0:T(8,128)S(1)}, f32[392,128]{1,0:T(8,128)S(1)}) custom-call(f32[2,128,128]{2,1,0:T(8,128)S(1)} %get-tuple-element.45.refs_0_, f32[2,128,128]{2,1,0:T(8,128)S(1)} %collective-permute-done.12.refs_1_, f32[2,128,128]{2,1,0:T(8,128)S(1)} %collective-permute-done.13.refs_2_, ...), custom_call_target="tpu_custom_call" | custom-call | tf_op jit(solution)/shard_map/pallas_call | solution.py:259
  39.3 8.4 %collective-permute-done.8.refs_2_ = f32[2,128,128]{2,1,0:T(8,128)S(1)} collective-permute-done((f32[2,128,128]{2,1,0:T(8,128)S(1)}, f32[2,128,128]{2,1,0:T(8,128)S(1)}, u32[]{:S(2)}, u32[]{:S(2)}) %collective-permute-start.8) | collective-permute-done | bytes 131104 | tf_op jit(solution)/shard_map/ppermute | solution.py:243
  47.8 2.3 %collective-permute-start.18 = (f32[264,128]{1,0:T(8,128)S(1)}, f32[264,128]{1,0:T(8,128)S(1)}, u32[]{:S(2)}, u32[]{:S(2)}) collective-permute-start(f32[264,128]{1,0:T(8,128)S(1)} %get-tuple-element.55), channel_id=1, source_target_pairs={{0,6},{1,7},{2,4},{3,5},{4,2},{5,3},{6,0},{7,1},{8,14},{9,15},{10,... | collective-permute-start | bytes 405512 | tf_op jit(solution)/shard_map/ppermute | solution.py:243
  50.2 1.6 %collective-permute-start.16 = (f32[264,128]{1,0:T(8,128)S(1)}, f32[264,128]{1,0:T(8,128)S(1)}, u32[]{:S(2)}, u32[]{:S(2)}) collective-permute-start(f32[264,128]{1,0:T(8,128)S(1)} %get-tuple-element.53), channel_id=1, source_target_pairs={{0,2},{1,3},{2,0},{3,1},{4,6},{5,7},{6,4},{7,5},{8,10},{9,11},{10,... | collective-permute-start | bytes 405512 | tf_op jit(solution)/shard_map/ppermute | solution.py:243
  52.3 3.8 %collective-permute-done.18.piece_ref = f32[264,128]{1,0:T(8,128)S(1)} collective-permute-done((f32[264,128]{1,0:T(8,128)S(1)}, f32[264,128]{1,0:T(8,128)S(1)}, u32[]{:S(2)}, u32[]{:S(2)}) %collective-permute-start.18) | collective-permute-done | bytes 135200 | tf_op jit(solution)/shard_map/ppermute | solution.py:243
  56.3 1.2 %collective-permute-done.19.refs_6_ = f32[136,128]{1,0:T(8,128)S(1)} collective-permute-done((f32[136,128]{1,0:T(8,128)S(1)}, f32[136,128]{1,0:T(8,128)S(1)}, u32[]{:S(2)}, u32[]{:S(2)}) %collective-permute-start.19) | collective-permute-done | bytes 69664 | tf_op jit(solution)/shard_map/ppermute | solution.py:243
  58.6 5.6 %collective-permute-done.17.refs_4_ = f32[264,128]{1,0:T(8,128)S(1)} collective-permute-done((f32[264,128]{1,0:T(8,128)S(1)}, f32[264,128]{1,0:T(8,128)S(1)}, u32[]{:S(2)}, u32[]{:S(2)}) %collective-permute-start.17) | collective-permute-done | bytes 135200 | tf_op jit(solution)/shard_map/ppermute | solution.py:243
  64.2 1.8 %shard_map.68 = (f32[128,16,128]{2,1,0:T(8,128)}, f32[1,4]{1,0:T(1,128)}) custom-call(f32[4,128,128]{2,1,0:T(8,128)S(1)} %get-tuple-element.43.refs_0_, f32[4,128,128]{2,1,0:T(8,128)S(1)} %collective-permute-done.10.refs_1_, f32[264,128]{1,0:T(8,128)S(1)} %get-tuple-element.52.refs_2_, f32[264,128]{1,0:T(8,128)S(1)} %collective-permute-done.16.refs_3_, ...), custom_call_target="tpu_custom_call" | custom-call | tf_op jit(solution)/shard_map/pallas_call | solution.py:259
  (34 shorter events, 5.4 us)
Async XLA Ops:
  1.7 7.0 %copy-start = (f32[1,3,128,128]{3,2,1,0:T(8,128)S(1)}, f32[1,3,128,128]{3,2,1,0:T(8,128)}, u32[]{:S(2)}) copy-start(f32[1,3,128,128]{3,2,1,0:T(8,128)} %param.5) | copy-start | bytes 589828
  1.7 19.0 %collective-permute-start.11 = (f32[128,8,128]{2,1,0:T(8,128)S(1)}, f32[128,8,128]{2,1,0:T(8,128)S(1)}, u32[]{:S(2)}, u32[]{:S(2)}) collective-permute-start(f32[128,8,128]{2,1,0:T(8,128)S(1)} %slice.4.x_ref), channel_id=1, source_target_pairs={{0,1},{1,0},{2,3},{3,2},{4,5},{5,4},{6,7},{7,6},{8,9},{9,8},{10,11... | collective-permute-start | bytes 1572872 | tf_op jit(solution)/shard_map/ppermute | solution.py:243
  3.5 9.0 %collective-permute-start = (f32[2,128,128]{2,1,0:T(8,128)S(1)}, f32[2,128,128]{2,1,0:T(8,128)S(1)}, u32[]{:S(2)}, u32[]{:S(2)}) collective-permute-start(f32[2,128,128]{2,1,0:T(8,128)S(1)} %get-tuple-element.32), channel_id=1, source_target_pairs={{0,2},{1,3},{2,0},{3,1},{4,6},{5,7},{6,4},{7,5},{8,10},{9,11},{10,... | collective-permute-start | bytes 393224 | tf_op jit(solution)/shard_map/ppermute | solution.py:243
  6.1 12.9 %collective-permute-start.1 = (f32[2,128,128]{2,1,0:T(8,128)S(1)}, f32[2,128,128]{2,1,0:T(8,128)S(1)}, u32[]{:S(2)}, u32[]{:S(2)}) collective-permute-start(f32[2,128,128]{2,1,0:T(8,128)S(1)} %get-tuple-element.33), channel_id=1, source_target_pairs={{0,4},{1,5},{2,6},{3,7},{4,0},{5,1},{6,2},{7,3},{8,12},{9,13},{10,... | collective-permute-start | bytes 393224 | tf_op jit(solution)/shard_map/ppermute | solution.py:243
  8.7 10.3 %collective-permute-start.2 = (f32[2,128,128]{2,1,0:T(8,128)S(1)}, f32[2,128,128]{2,1,0:T(8,128)S(1)}, u32[]{:S(2)}, u32[]{:S(2)}) collective-permute-start(f32[2,128,128]{2,1,0:T(8,128)S(1)} %get-tuple-element.34), channel_id=1, source_target_pairs={{0,6},{1,7},{2,4},{3,5},{4,2},{5,3},{6,0},{7,1},{8,14},{9,15},{10,... | collective-permute-start | bytes 393224 | tf_op jit(solution)/shard_map/ppermute | solution.py:243
  8.7 14.8 %collective-permute-start.6 = (f32[3,128,128]{2,1,0:T(8,128)S(1)}, f32[3,128,128]{2,1,0:T(8,128)S(1)}, u32[]{:S(2)}, u32[]{:S(2)}) collective-permute-start(f32[3,128,128]{2,1,0:T(8,128)S(1)} %bitcast.4), channel_id=1, source_target_pairs={{0,24},{8,16},{16,8},{24,0},{1,25},{9,17},{17,9},{25,1},{2,26},{10... | collective-permute-start | bytes 589832 | tf_op jit(solution)/shard_map/ppermute | solution.py:243
  12.4 12.2 %collective-permute-start.5 = (f32[3,128,128]{2,1,0:T(8,128)S(1)}, f32[3,128,128]{2,1,0:T(8,128)S(1)}, u32[]{:S(2)}, u32[]{:S(2)}) collective-permute-start(f32[3,128,128]{2,1,0:T(8,128)S(1)} %bitcast.5), channel_id=1, source_target_pairs={{0,16},{8,24},{16,0},{24,8},{1,17},{9,25},{17,1},{25,9},{2,18},{10... | collective-permute-start | bytes 589832 | tf_op jit(solution)/shard_map/ppermute | solution.py:243
  19.1 9.7 %collective-permute-start.3 = (f32[4,128,128]{2,1,0:T(8,128)S(1)}, f32[4,128,128]{2,1,0:T(8,128)S(1)}, u32[]{:S(2)}, u32[]{:S(2)}) collective-permute-start(f32[4,128,128]{2,1,0:T(8,128)S(1)} %get-tuple-element.36), channel_id=1, source_target_pairs={{0,1},{1,0},{2,3},{3,2},{4,5},{5,4},{6,7},{7,6},{8,9},{9,8},{10,11... | collective-permute-start | bytes 786440 | tf_op jit(solution)/shard_map/ppermute | solution.py:243
  19.2 7.3 %collective-permute-start.4 = (f32[3,128,128]{2,1,0:T(8,128)S(1)}, f32[3,128,128]{2,1,0:T(8,128)S(1)}, u32[]{:S(2)}, u32[]{:S(2)}) collective-permute-start(f32[3,128,128]{2,1,0:T(8,128)S(1)} %bitcast.6), channel_id=1, source_target_pairs={{0,8},{8,0},{16,24},{24,16},{1,9},{9,1},{17,25},{25,17},{2,10},{10... | collective-permute-start | bytes 589832 | tf_op jit(solution)/shard_map/ppermute | solution.py:243
  20.9 5.2 %copy-start.2 = (s32[1,4,3,7]{3,1,2,0:T(4,128)S(1)}, s32[1,4,3,7]{3,1,2,0:T(4,128)}, u32[]{:S(2)}) copy-start(s32[1,4,3,7]{3,1,2,0:T(4,128)} %param.6) | copy-start | bytes 1012
  20.9 13.7 %collective-permute-start.12 = (f32[2,128,128]{2,1,0:T(8,128)S(1)}, f32[2,128,128]{2,1,0:T(8,128)S(1)}, u32[]{:S(2)}, u32[]{:S(2)}) collective-permute-start(f32[2,128,128]{2,1,0:T(8,128)S(1)} %get-tuple-element.46), channel_id=1, source_target_pairs={{0,2},{1,3},{2,0},{3,1},{4,6},{5,7},{6,4},{7,5},{8,10},{9,11},{10,... | collective-permute-start | bytes 393224 | tf_op jit(solution)/shard_map/ppermute | solution.py:243
  23.5 12.9 %collective-permute-start.13 = (f32[2,128,128]{2,1,0:T(8,128)S(1)}, f32[2,128,128]{2,1,0:T(8,128)S(1)}, u32[]{:S(2)}, u32[]{:S(2)}) collective-permute-start(f32[2,128,128]{2,1,0:T(8,128)S(1)} %get-tuple-element.47), channel_id=1, source_target_pairs={{0,4},{1,5},{2,6},{3,7},{4,0},{5,1},{6,2},{7,3},{8,12},{9,13},{10,... | collective-permute-start | bytes 393224 | tf_op jit(solution)/shard_map/ppermute | solution.py:243
  24.6 11.8 %collective-permute-start.14 = (f32[2,128,128]{2,1,0:T(8,128)S(1)}, f32[2,128,128]{2,1,0:T(8,128)S(1)}, u32[]{:S(2)}, u32[]{:S(2)}) collective-permute-start(f32[2,128,128]{2,1,0:T(8,128)S(1)} %get-tuple-element.48), channel_id=1, source_target_pairs={{0,6},{1,7},{2,4},{3,5},{4,2},{5,3},{6,0},{7,1},{8,14},{9,15},{10,... | collective-permute-start | bytes 393224 | tf_op jit(solution)/shard_map/ppermute | solution.py:243
  26.1 0.7 %copy-start.1 = (s32[4,3]{1,0:T(4,128)S(1)}, s32[4,3]{1,0:T(4,128)}, u32[]{:S(2)}) copy-start(s32[4,3]{1,0:T(4,128)} %targets_ref.1) | copy-start | bytes 148
  31.1 8.2 %collective-permute-start.7 = (f32[2,128,128]{2,1,0:T(8,128)S(1)}, f32[2,128,128]{2,1,0:T(8,128)S(1)}, u32[]{:S(2)}, u32[]{:S(2)}) collective-permute-start(f32[2,128,128]{2,1,0:T(8,128)S(1)} %get-tuple-element.40), channel_id=1, source_target_pairs={{0,2},{1,3},{2,0},{3,1},{4,6},{5,7},{6,4},{7,5},{8,10},{9,11},{10,... | collective-permute-start | bytes 393224 | tf_op jit(solution)/shard_map/ppermute | solution.py:243
  33.5 14.2 %collective-permute-start.8 = (f32[2,128,128]{2,1,0:T(8,128)S(1)}, f32[2,128,128]{2,1,0:T(8,128)S(1)}, u32[]{:S(2)}, u32[]{:S(2)}) collective-permute-start(f32[2,128,128]{2,1,0:T(8,128)S(1)} %get-tuple-element.41), channel_id=1, source_target_pairs={{0,4},{1,5},{2,6},{3,7},{4,0},{5,1},{6,2},{7,3},{8,12},{9,13},{10,... | collective-permute-start | bytes 393224 | tf_op jit(solution)/shard_map/ppermute | solution.py:243
  34.6 13.1 %collective-permute-start.9 = (f32[2,128,128]{2,1,0:T(8,128)S(1)}, f32[2,128,128]{2,1,0:T(8,128)S(1)}, u32[]{:S(2)}, u32[]{:S(2)}) collective-permute-start(f32[2,128,128]{2,1,0:T(8,128)S(1)} %get-tuple-element.42), channel_id=1, source_target_pairs={{0,6},{1,7},{2,4},{3,5},{4,2},{5,3},{6,0},{7,1},{8,14},{9,15},{10,... | collective-permute-start | bytes 393224 | tf_op jit(solution)/shard_map/ppermute | solution.py:243
  38.8 11.4 %collective-permute-start.15 = (f32[392,128]{1,0:T(8,128)S(1)}, f32[392,128]{1,0:T(8,128)S(1)}, u32[]{:S(2)}, u32[]{:S(2)}) collective-permute-start(f32[392,128]{1,0:T(8,128)S(1)} %get-tuple-element.51), channel_id=1, source_target_pairs={{0,1},{1,0},{2,3},{3,2},{4,5},{5,4},{6,7},{7,6},{8,9},{9,8},{10,11... | collective-permute-start | bytes 602120 | tf_op jit(solution)/shard_map/ppermute | solution.py:243
  47.7 8.5 %collective-permute-start.10 = (f32[4,128,128]{2,1,0:T(8,128)S(1)}, f32[4,128,128]{2,1,0:T(8,128)S(1)}, u32[]{:S(2)}, u32[]{:S(2)}) collective-permute-start(f32[4,128,128]{2,1,0:T(8,128)S(1)} %get-tuple-element.44), channel_id=1, source_target_pairs={{0,1},{1,0},{2,3},{3,2},{4,5},{5,4},{6,7},{7,6},{8,9},{9,8},{10,11... | collective-permute-start | bytes 786440 | tf_op jit(solution)/shard_map/ppermute | solution.py:243
  47.8 8.4 %collective-permute-start.18 = (f32[264,128]{1,0:T(8,128)S(1)}, f32[264,128]{1,0:T(8,128)S(1)}, u32[]{:S(2)}, u32[]{:S(2)}) collective-permute-start(f32[264,128]{1,0:T(8,128)S(1)} %get-tuple-element.55), channel_id=1, source_target_pairs={{0,6},{1,7},{2,4},{3,5},{4,2},{5,3},{6,0},{7,1},{8,14},{9,15},{10,... | collective-permute-start | bytes 405512 | tf_op jit(solution)/shard_map/ppermute | solution.py:243
  50.2 8.4 %collective-permute-start.16 = (f32[264,128]{1,0:T(8,128)S(1)}, f32[264,128]{1,0:T(8,128)S(1)}, u32[]{:S(2)}, u32[]{:S(2)}) collective-permute-start(f32[264,128]{1,0:T(8,128)S(1)} %get-tuple-element.53), channel_id=1, source_target_pairs={{0,2},{1,3},{2,0},{3,1},{4,6},{5,7},{6,4},{7,5},{8,10},{9,11},{10,... | collective-permute-start | bytes 405512 | tf_op jit(solution)/shard_map/ppermute | solution.py:243
  51.8 12.4 %collective-permute-start.17 = (f32[264,128]{1,0:T(8,128)S(1)}, f32[264,128]{1,0:T(8,128)S(1)}, u32[]{:S(2)}, u32[]{:S(2)}) collective-permute-start(f32[264,128]{1,0:T(8,128)S(1)} %get-tuple-element.54), channel_id=1, source_target_pairs={{0,4},{1,5},{2,6},{3,7},{4,0},{5,1},{6,2},{7,3},{8,12},{9,13},{10,... | collective-permute-start | bytes 405512 | tf_op jit(solution)/shard_map/ppermute | solution.py:243
  56.2 1.3 %collective-permute-start.19 = (f32[136,128]{1,0:T(8,128)S(1)}, f32[136,128]{1,0:T(8,128)S(1)}, u32[]{:S(2)}, u32[]{:S(2)}) collective-permute-start(f32[136,128]{1,0:T(8,128)S(1)} %get-tuple-element.57), channel_id=1, source_target_pairs={{0,1},{1,0},{2,3},{3,2},{4,5},{5,4},{6,7},{7,6},{8,9},{9,8},{10,11... | collective-permute-start | bytes 208904 | tf_op jit(solution)/shard_map/ppermute | solution.py:243

commit v2 on v1

--- a/solution.py
+++ b/solution.py
@@ -16,6 +16,7 @@
 SMEM = pl.BlockSpec(memory_space=pltpu.SMEM)
 EXTRA = 8
 STEPS = 4
+OUT_STEPS = 8
 VMEM_LIMIT = 12 * 2**20
 
 
@@ -201,7 +202,7 @@
 
 def unpack_kernel(lines, early, steps, total_amps, *refs):
     held, refs = refs[: 2 * early], refs[2 * early :]
-    joined, far_refs, (x_ref, logs_ref, out, sems) = refs[: lines - 1], refs[lines - 1 : lines + 1], refs[lines + 1 :]
+    joined, far_refs, (x_ref, logs_ref, out, logs_held, sems) = refs[: lines - 1], refs[lines - 1 : lines + 1], refs[lines + 1 :]
     me = lax.axis_index("amp")
     register, middle, lanes = out.shape
     sections = logs_ref.shape[1]
@@ -232,7 +233,9 @@
     logs = jnp.log(totals[1 : sections + 1] / totals[:sections])
     rows = lax.broadcasted_iota(jnp.int32, (sections, sections), 0)
     columns = lax.broadcasted_iota(jnp.int32, (sections, sections), 1)
-    logs_ref[...] = jnp.sum(jnp.where(rows == columns, logs, 0.0), axis=0, keepdims=True)
+    logs_held[...] = jnp.sum(jnp.where(rows == columns, logs, 0.0), axis=0, keepdims=True)
+    copies.append(pltpu.make_async_copy(logs_held, logs_ref, sems.at[steps]))
+    copies[-1].start()
     for copy in copies:
         copy.wait()
 
@@ -323,11 +326,15 @@
             held += [near, across(other)]
 
     out, logs = kernel(
-        functools.partial(unpack_kernel, lines, chunks - 1, STEPS, float(amp_local * amp)),
+        functools.partial(unpack_kernel, lines, chunks - 1, OUT_STEPS, float(amp_local * amp)),
         [array(register, middle, register), array(1, sections)],
         *held,
-        out_specs=[pl.BlockSpec(memory_space=pltpu.HBM), VMEM],
-        scratch_shapes=[pltpu.VMEM((register, middle, register), F32), pltpu.SemaphoreType.DMA((STEPS,))],
+        out_specs=[pl.BlockSpec(memory_space=pltpu.HBM)] * 2,
+        scratch_shapes=[
+            pltpu.VMEM((register, middle, register), F32),
+            pltpu.VMEM((1, sections), F32),
+            pltpu.SemaphoreType.DMA((OUT_STEPS + 1,)),
+        ],
     )
     return out.reshape(1, amp_local), logs
 

time: 66.2 us -> 65.6 us (level)
  no operation moved by 1% of the time
where the time goes in v2:
time: 65.6 us; the launch traced here: 65.4 us
  waiting for transfers between devices  27.4 us (42%)
  starting transfers between devices  26.6 us (41%)
  Pallas kernels  9.21 us (14%)
  local copies, waits for them, and re-layouts  1.39 us (2%)
  between operations  0.77 us (1%)
    ppermute x20, waiting for transfers between devices, swap(): return lax.ppermute(piece, axis, [(i, i ^ k) for i in range(size)])  27.4 us
    ppermute x20, starting transfers between devices, swap(): return lax.ppermute(piece, axis, [(i, i ^ k) for i in range(size)])  26.6 us
    pallas_call x10, Pallas kernels, kernel(): pl.pallas_call(body, out_shape=out_shape, compiler_params=params, **{**sp...  9.21 us
  transfers between devices with their start and end apart: 20, of which 10 were waited for; matrix products, arithmetic and copies ran while one was open for 0% of the time, Pallas kernels for 12%

profile of v2, /device:TPU:0, one launch (start us, length us, event | category | flops | bytes accessed | tf_op | source)
XLA Modules:
  0.0 65.4 jit_solution(11209107513018567080)
XLA Ops:
  0.6 1.1 %slice.4.x_ref = f32[128,8,128]{2,1,0:T(8,128)S(1)} slice(f32[128,16,128]{2,1,0:T(8,128)} %bitcast.8), slice={[0:128], [8:16], [0:128]} | slice | bytes 1048576 | tf_op jit(solution)/shard_map/slice | solution.py:287
  2.3 1.2 %shard_map.59 = (f32[2,128,128]{2,1,0:T(8,128)S(1)}, f32[2,128,128]{2,1,0:T(8,128)S(1)}, f32[2,128,128]{2,1,0:T(8,128)S(1)}, f32[2,128,128]{2,1,0:T(8,128)S(1)}) custom-call(f32[128,16,128]{2,1,0:T(8,128)} %bitcast.9), custom_call_target="tpu_custom_call" | custom-call | tf_op jit(solution)/shard_map/pallas_call | solution.py:262
  3.5 2.7 %collective-permute-start = (f32[2,128,128]{2,1,0:T(8,128)S(1)}, f32[2,128,128]{2,1,0:T(8,128)S(1)}, u32[]{:S(2)}, u32[]{:S(2)}) collective-permute-start(f32[2,128,128]{2,1,0:T(8,128)S(1)} %get-tuple-element.32), channel_id=1, source_target_pairs={{0,2},{1,3},{2,0},{3,1},{4,6},{5,7},{6,4},{7,5},{8,10},{9,11},{10,... | collective-permute-start | bytes 393224 | tf_op jit(solution)/shard_map/ppermute | solution.py:246
  6.1 2.6 %collective-permute-start.1 = (f32[2,128,128]{2,1,0:T(8,128)S(1)}, f32[2,128,128]{2,1,0:T(8,128)S(1)}, u32[]{:S(2)}, u32[]{:S(2)}) collective-permute-start(f32[2,128,128]{2,1,0:T(8,128)S(1)} %get-tuple-element.33), channel_id=1, source_target_pairs={{0,4},{1,5},{2,6},{3,7},{4,0},{5,1},{6,2},{7,3},{8,12},{9,13},{10,... | collective-permute-start | bytes 393224 | tf_op jit(solution)/shard_map/ppermute | solution.py:246
  8.7 2.7 %collective-permute-start.6 = (f32[3,128,128]{2,1,0:T(8,128)S(1)}, f32[3,128,128]{2,1,0:T(8,128)S(1)}, u32[]{:S(2)}, u32[]{:S(2)}) collective-permute-start(f32[3,128,128]{2,1,0:T(8,128)S(1)} %bitcast.4), channel_id=1, source_target_pairs={{0,24},{8,16},{16,8},{24,0},{1,25},{9,17},{17,9},{25,1},{2,26},{10... | collective-permute-start | bytes 589832 | tf_op jit(solution)/shard_map/ppermute | solution.py:246
  12.4 1.7 %collective-permute-start.5 = (f32[3,128,128]{2,1,0:T(8,128)S(1)}, f32[3,128,128]{2,1,0:T(8,128)S(1)}, u32[]{:S(2)}, u32[]{:S(2)}) collective-permute-start(f32[3,128,128]{2,1,0:T(8,128)S(1)} %bitcast.5), channel_id=1, source_target_pairs={{0,16},{8,24},{16,0},{24,8},{1,17},{9,25},{17,1},{25,9},{2,18},{10... | collective-permute-start | bytes 589832 | tf_op jit(solution)/shard_map/ppermute | solution.py:246
  14.2 4.9 %collective-permute-done.1.refs_2_ = f32[2,128,128]{2,1,0:T(8,128)S(1)} collective-permute-done((f32[2,128,128]{2,1,0:T(8,128)S(1)}, f32[2,128,128]{2,1,0:T(8,128)S(1)}, u32[]{:S(2)}, u32[]{:S(2)}) %collective-permute-start.1) | collective-permute-done | bytes 131104 | tf_op jit(solution)/shard_map/ppermute | solution.py:246
  19.2 1.6 %collective-permute-start.4 = (f32[3,128,128]{2,1,0:T(8,128)S(1)}, f32[3,128,128]{2,1,0:T(8,128)S(1)}, u32[]{:S(2)}, u32[]{:S(2)}) collective-permute-start(f32[3,128,128]{2,1,0:T(8,128)S(1)} %bitcast.6), channel_id=1, source_target_pairs={{0,8},{8,0},{16,24},{24,16},{1,9},{9,1},{17,25},{25,17},{2,10},{10... | collective-permute-start | bytes 589832 | tf_op jit(solution)/shard_map/ppermute | solution.py:246
  20.9 2.6 %collective-permute-start.12 = (f32[2,128,128]{2,1,0:T(8,128)S(1)}, f32[2,128,128]{2,1,0:T(8,128)S(1)}, u32[]{:S(2)}, u32[]{:S(2)}) collective-permute-start(f32[2,128,128]{2,1,0:T(8,128)S(1)} %get-tuple-element.46), channel_id=1, source_target_pairs={{0,2},{1,3},{2,0},{3,1},{4,6},{5,7},{6,4},{7,5},{8,10},{9,11},{10,... | collective-permute-start | bytes 393224 | tf_op jit(solution)/shard_map/ppermute | solution.py:246
  23.5 1.1 %collective-permute-start.13 = (f32[2,128,128]{2,1,0:T(8,128)S(1)}, f32[2,128,128]{2,1,0:T(8,128)S(1)}, u32[]{:S(2)}, u32[]{:S(2)}) collective-permute-start(f32[2,128,128]{2,1,0:T(8,128)S(1)} %get-tuple-element.47), channel_id=1, source_target_pairs={{0,4},{1,5},{2,6},{3,7},{4,0},{5,1},{6,2},{7,3},{8,12},{9,13},{10,... | collective-permute-start | bytes 393224 | tf_op jit(solution)/shard_map/ppermute | solution.py:246
  24.6 1.4 %collective-permute-start.14 = (f32[2,128,128]{2,1,0:T(8,128)S(1)}, f32[2,128,128]{2,1,0:T(8,128)S(1)}, u32[]{:S(2)}, u32[]{:S(2)}) collective-permute-start(f32[2,128,128]{2,1,0:T(8,128)S(1)} %get-tuple-element.48), channel_id=1, source_target_pairs={{0,6},{1,7},{2,4},{3,5},{4,2},{5,3},{6,0},{7,1},{8,14},{9,15},{10,... | collective-permute-start | bytes 393224 | tf_op jit(solution)/shard_map/ppermute | solution.py:246
  26.8 2.0 %shard_map.61 = (bf16[4,256,256]{2,1,0:T(8,128)(2,1)S(1)}, bf16[4,256,256]{2,1,0:T(8,128)(2,1)S(1)}) custom-call(s32[4,3,7]{2,1,0:T(4,128)S(1)} %copy.6.picks_ref, s32[4,3]{1,0:T(4,128)S(1)} %copy-done.1, f32[3,128,128]{2,1,0:T(8,128)S(1)} %bitcast.7, f32[3,128,128]{2,1,0:T(8,128)S(1)} %collective-permute-done.4.refs_1_, ...), custom_call_target="tpu_custom_call" | custom-call | tf_op jit(solution)/shard_map/pallas_call | solution.py:262
  28.8 2.3 %shard_map.62 = (f32[2,128,128]{2,1,0:T(8,128)S(1)}, f32[2,128,128]{2,1,0:T(8,128)S(1)}, f32[2,128,128]{2,1,0:T(8,128)S(1)}, f32[2,128,128]{2,1,0:T(8,128)S(1)}, f32[8,128]{1,0:T(8,128)S(1)}) custom-call(f32[4,128,128]{2,1,0:T(8,128)S(1)} %get-tuple-element.35.refs_0_, f32[4,128,128]{2,1,0:T(8,128)S(1)} %collective-permute-done.3.refs_1_, ...), custom_call_target="tpu_custom_call" | custom-call | tf_op jit(solution)/shard_map/pallas_call | solution.py:262
  31.1 2.4 %collective-permute-start.7 = (f32[2,128,128]{2,1,0:T(8,128)S(1)}, f32[2,128,128]{2,1,0:T(8,128)S(1)}, u32[]{:S(2)}, u32[]{:S(2)}) collective-permute-start(f32[2,128,128]{2,1,0:T(8,128)S(1)} %get-tuple-element.40), channel_id=1, source_target_pairs={{0,2},{1,3},{2,0},{3,1},{4,6},{5,7},{6,4},{7,5},{8,10},{9,11},{10,... | collective-permute-start | bytes 393224 | tf_op jit(solution)/shard_map/ppermute | solution.py:246
  33.5 1.1 %collective-permute-start.8 = (f32[2,128,128]{2,1,0:T(8,128)S(1)}, f32[2,128,128]{2,1,0:T(8,128)S(1)}, u32[]{:S(2)}, u32[]{:S(2)}) collective-permute-start(f32[2,128,128]{2,1,0:T(8,128)S(1)} %get-tuple-element.41), channel_id=1, source_target_pairs={{0,4},{1,5},{2,6},{3,7},{4,0},{5,1},{6,2},{7,3},{8,12},{9,13},{10,... | collective-permute-start | bytes 393224 | tf_op jit(solution)/shard_map/ppermute | solution.py:246
  34.6 1.4 %collective-permute-start.9 = (f32[2,128,128]{2,1,0:T(8,128)S(1)}, f32[2,128,128]{2,1,0:T(8,128)S(1)}, u32[]{:S(2)}, u32[]{:S(2)}) collective-permute-start(f32[2,128,128]{2,1,0:T(8,128)S(1)} %get-tuple-element.42), channel_id=1, source_target_pairs={{0,6},{1,7},{2,4},{3,5},{4,2},{5,3},{6,0},{7,1},{8,14},{9,15},{10,... | collective-permute-start | bytes 393224 | tf_op jit(solution)/shard_map/ppermute | solution.py:246
  36.4 2.3 %shard_map.65 = (f32[264,128]{1,0:T(8,128)S(1)}, f32[392,128]{1,0:T(8,128)S(1)}, f32[392,128]{1,0:T(8,128)S(1)}) custom-call(f32[2,128,128]{2,1,0:T(8,128)S(1)} %get-tuple-element.45.refs_0_, f32[2,128,128]{2,1,0:T(8,128)S(1)} %collective-permute-done.12.refs_1_, f32[2,128,128]{2,1,0:T(8,128)S(1)} %collective-permute-done.13.refs_2_, ...), custom_call_target="tpu_custom_call" | custom-call | tf_op jit(solution)/shard_map/pallas_call | solution.py:262
  39.3 8.4 %collective-permute-done.8.refs_2_ = f32[2,128,128]{2,1,0:T(8,128)S(1)} collective-permute-done((f32[2,128,128]{2,1,0:T(8,128)S(1)}, f32[2,128,128]{2,1,0:T(8,128)S(1)}, u32[]{:S(2)}, u32[]{:S(2)}) %collective-permute-start.8) | collective-permute-done | bytes 131104 | tf_op jit(solution)/shard_map/ppermute | solution.py:246
  47.8 2.3 %collective-permute-start.18 = (f32[264,128]{1,0:T(8,128)S(1)}, f32[264,128]{1,0:T(8,128)S(1)}, u32[]{:S(2)}, u32[]{:S(2)}) collective-permute-start(f32[264,128]{1,0:T(8,128)S(1)} %get-tuple-element.55), channel_id=1, source_target_pairs={{0,6},{1,7},{2,4},{3,5},{4,2},{5,3},{6,0},{7,1},{8,14},{9,15},{10,... | collective-permute-start | bytes 405512 | tf_op jit(solution)/shard_map/ppermute | solution.py:246
  50.2 1.6 %collective-permute-start.16 = (f32[264,128]{1,0:T(8,128)S(1)}, f32[264,128]{1,0:T(8,128)S(1)}, u32[]{:S(2)}, u32[]{:S(2)}) collective-permute-start(f32[264,128]{1,0:T(8,128)S(1)} %get-tuple-element.53), channel_id=1, source_target_pairs={{0,2},{1,3},{2,0},{3,1},{4,6},{5,7},{6,4},{7,5},{8,10},{9,11},{10,... | collective-permute-start | bytes 405512 | tf_op jit(solution)/shard_map/ppermute | solution.py:246
  52.3 3.8 %collective-permute-done.18.piece_ref = f32[264,128]{1,0:T(8,128)S(1)} collective-permute-done((f32[264,128]{1,0:T(8,128)S(1)}, f32[264,128]{1,0:T(8,128)S(1)}, u32[]{:S(2)}, u32[]{:S(2)}) %collective-permute-start.18) | collective-permute-done | bytes 135200 | tf_op jit(solution)/shard_map/ppermute | solution.py:246
  56.3 1.2 %collective-permute-done.19.refs_6_ = f32[136,128]{1,0:T(8,128)S(1)} collective-permute-done((f32[136,128]{1,0:T(8,128)S(1)}, f32[136,128]{1,0:T(8,128)S(1)}, u32[]{:S(2)}, u32[]{:S(2)}) %collective-permute-start.19) | collective-permute-done | bytes 69664 | tf_op jit(solution)/shard_map/ppermute | solution.py:246
  58.6 5.6 %collective-permute-done.17.refs_4_ = f32[264,128]{1,0:T(8,128)S(1)} collective-permute-done((f32[264,128]{1,0:T(8,128)S(1)}, f32[264,128]{1,0:T(8,128)S(1)}, u32[]{:S(2)}, u32[]{:S(2)}) %collective-permute-start.17) | collective-permute-done | bytes 135200 | tf_op jit(solution)/shard_map/ppermute | solution.py:246
  64.2 1.2 %shard_map.68 = (f32[128,16,128]{2,1,0:T(8,128)}, f32[1,4]{1,0:T(1,128)}) custom-call(f32[4,128,128]{2,1,0:T(8,128)S(1)} %get-tuple-element.43.refs_0_, f32[4,128,128]{2,1,0:T(8,128)S(1)} %collective-permute-done.10.refs_1_, f32[264,128]{1,0:T(8,128)S(1)} %get-tuple-element.52.refs_2_, f32[264,128]{1,0:T(8,128)S(1)} %collective-permute-done.16.refs_3_, ...), custom_call_target="tpu_custom_call" | custom-call | tf_op jit(solution)/shard_map/pallas_call | solution.py:262
  (34 shorter events, 5.4 us)
Async XLA Ops:
  1.7 7.0 %copy-start = (f32[1,3,128,128]{3,2,1,0:T(8,128)S(1)}, f32[1,3,128,128]{3,2,1,0:T(8,128)}, u32[]{:S(2)}) copy-start(f32[1,3,128,128]{3,2,1,0:T(8,128)} %param.5) | copy-start | bytes 589828
  1.7 19.0 %collective-permute-start.11 = (f32[128,8,128]{2,1,0:T(8,128)S(1)}, f32[128,8,128]{2,1,0:T(8,128)S(1)}, u32[]{:S(2)}, u32[]{:S(2)}) collective-permute-start(f32[128,8,128]{2,1,0:T(8,128)S(1)} %slice.4.x_ref), channel_id=1, source_target_pairs={{0,1},{1,0},{2,3},{3,2},{4,5},{5,4},{6,7},{7,6},{8,9},{9,8},{10,11... | collective-permute-start | bytes 1572872 | tf_op jit(solution)/shard_map/ppermute | solution.py:246
  3.5 9.0 %collective-permute-start = (f32[2,128,128]{2,1,0:T(8,128)S(1)}, f32[2,128,128]{2,1,0:T(8,128)S(1)}, u32[]{:S(2)}, u32[]{:S(2)}) collective-permute-start(f32[2,128,128]{2,1,0:T(8,128)S(1)} %get-tuple-element.32), channel_id=1, source_target_pairs={{0,2},{1,3},{2,0},{3,1},{4,6},{5,7},{6,4},{7,5},{8,10},{9,11},{10,... | collective-permute-start | bytes 393224 | tf_op jit(solution)/shard_map/ppermute | solution.py:246
  6.1 12.9 %collective-permute-start.1 = (f32[2,128,128]{2,1,0:T(8,128)S(1)}, f32[2,128,128]{2,1,0:T(8,128)S(1)}, u32[]{:S(2)}, u32[]{:S(2)}) collective-permute-start(f32[2,128,128]{2,1,0:T(8,128)S(1)} %get-tuple-element.33), channel_id=1, source_target_pairs={{0,4},{1,5},{2,6},{3,7},{4,0},{5,1},{6,2},{7,3},{8,12},{9,13},{10,... | collective-permute-start | bytes 393224 | tf_op jit(solution)/shard_map/ppermute | solution.py:246
  8.7 10.3 %collective-permute-start.2 = (f32[2,128,128]{2,1,0:T(8,128)S(1)}, f32[2,128,128]{2,1,0:T(8,128)S(1)}, u32[]{:S(2)}, u32[]{:S(2)}) collective-permute-start(f32[2,128,128]{2,1,0:T(8,128)S(1)} %get-tuple-element.34), channel_id=1, source_target_pairs={{0,6},{1,7},{2,4},{3,5},{4,2},{5,3},{6,0},{7,1},{8,14},{9,15},{10,... | collective-permute-start | bytes 393224 | tf_op jit(solution)/shard_map/ppermute | solution.py:246
  8.7 14.8 %collective-permute-start.6 = (f32[3,128,128]{2,1,0:T(8,128)S(1)}, f32[3,128,128]{2,1,0:T(8,128)S(1)}, u32[]{:S(2)}, u32[]{:S(2)}) collective-permute-start(f32[3,128,128]{2,1,0:T(8,128)S(1)} %bitcast.4), channel_id=1, source_target_pairs={{0,24},{8,16},{16,8},{24,0},{1,25},{9,17},{17,9},{25,1},{2,26},{10... | collective-permute-start | bytes 589832 | tf_op jit(solution)/shard_map/ppermute | solution.py:246
  12.4 12.2 %collective-permute-start.5 = (f32[3,128,128]{2,1,0:T(8,128)S(1)}, f32[3,128,128]{2,1,0:T(8,128)S(1)}, u32[]{:S(2)}, u32[]{:S(2)}) collective-permute-start(f32[3,128,128]{2,1,0:T(8,128)S(1)} %bitcast.5), channel_id=1, source_target_pairs={{0,16},{8,24},{16,0},{24,8},{1,17},{9,25},{17,1},{25,9},{2,18},{10... | collective-permute-start | bytes 589832 | tf_op jit(solution)/shard_map/ppermute | solution.py:246
  19.1 9.7 %collective-permute-start.3 = (f32[4,128,128]{2,1,0:T(8,128)S(1)}, f32[4,128,128]{2,1,0:T(8,128)S(1)}, u32[]{:S(2)}, u32[]{:S(2)}) collective-permute-start(f32[4,128,128]{2,1,0:T(8,128)S(1)} %get-tuple-element.36), channel_id=1, source_target_pairs={{0,1},{1,0},{2,3},{3,2},{4,5},{5,4},{6,7},{7,6},{8,9},{9,8},{10,11... | collective-permute-start | bytes 786440 | tf_op jit(solution)/shard_map/ppermute | solution.py:246
  19.2 7.3 %collective-permute-start.4 = (f32[3,128,128]{2,1,0:T(8,128)S(1)}, f32[3,128,128]{2,1,0:T(8,128)S(1)}, u32[]{:S(2)}, u32[]{:S(2)}) collective-permute-start(f32[3,128,128]{2,1,0:T(8,128)S(1)} %bitcast.6), channel_id=1, source_target_pairs={{0,8},{8,0},{16,24},{24,16},{1,9},{9,1},{17,25},{25,17},{2,10},{10... | collective-permute-start | bytes 589832 | tf_op jit(solution)/shard_map/ppermute | solution.py:246
  20.9 5.2 %copy-start.2 = (s32[1,4,3,7]{3,1,2,0:T(4,128)S(1)}, s32[1,4,3,7]{3,1,2,0:T(4,128)}, u32[]{:S(2)}) copy-start(s32[1,4,3,7]{3,1,2,0:T(4,128)} %param.6) | copy-start | bytes 1012
  20.9 13.7 %collective-permute-start.12 = (f32[2,128,128]{2,1,0:T(8,128)S(1)}, f32[2,128,128]{2,1,0:T(8,128)S(1)}, u32[]{:S(2)}, u32[]{:S(2)}) collective-permute-start(f32[2,128,128]{2,1,0:T(8,128)S(1)} %get-tuple-element.46), channel_id=1, source_target_pairs={{0,2},{1,3},{2,0},{3,1},{4,6},{5,7},{6,4},{7,5},{8,10},{9,11},{10,... | collective-permute-start | bytes 393224 | tf_op jit(solution)/shard_map/ppermute | solution.py:246
  23.5 12.9 %collective-permute-start.13 = (f32[2,128,128]{2,1,0:T(8,128)S(1)}, f32[2,128,128]{2,1,0:T(8,128)S(1)}, u32[]{:S(2)}, u32[]{:S(2)}) collective-permute-start(f32[2,128,128]{2,1,0:T(8,128)S(1)} %get-tuple-element.47), channel_id=1, source_target_pairs={{0,4},{1,5},{2,6},{3,7},{4,0},{5,1},{6,2},{7,3},{8,12},{9,13},{10,... | collective-permute-start | bytes 393224 | tf_op jit(solution)/shard_map/ppermute | solution.py:246
  24.6 11.8 %collective-permute-start.14 = (f32[2,128,128]{2,1,0:T(8,128)S(1)}, f32[2,128,128]{2,1,0:T(8,128)S(1)}, u32[]{:S(2)}, u32[]{:S(2)}) collective-permute-start(f32[2,128,128]{2,1,0:T(8,128)S(1)} %get-tuple-element.48), channel_id=1, source_target_pairs={{0,6},{1,7},{2,4},{3,5},{4,2},{5,3},{6,0},{7,1},{8,14},{9,15},{10,... | collective-permute-start | bytes 393224 | tf_op jit(solution)/shard_map/ppermute | solution.py:246
  26.1 0.7 %copy-start.1 = (s32[4,3]{1,0:T(4,128)S(1)}, s32[4,3]{1,0:T(4,128)}, u32[]{:S(2)}) copy-start(s32[4,3]{1,0:T(4,128)} %targets_ref.1) | copy-start | bytes 148
  31.1 8.2 %collective-permute-start.7 = (f32[2,128,128]{2,1,0:T(8,128)S(1)}, f32[2,128,128]{2,1,0:T(8,128)S(1)}, u32[]{:S(2)}, u32[]{:S(2)}) collective-permute-start(f32[2,128,128]{2,1,0:T(8,128)S(1)} %get-tuple-element.40), channel_id=1, source_target_pairs={{0,2},{1,3},{2,0},{3,1},{4,6},{5,7},{6,4},{7,5},{8,10},{9,11},{10,... | collective-permute-start | bytes 393224 | tf_op jit(solution)/shard_map/ppermute | solution.py:246
  33.5 14.2 %collective-permute-start.8 = (f32[2,128,128]{2,1,0:T(8,128)S(1)}, f32[2,128,128]{2,1,0:T(8,128)S(1)}, u32[]{:S(2)}, u32[]{:S(2)}) collective-permute-start(f32[2,128,128]{2,1,0:T(8,128)S(1)} %get-tuple-element.41), channel_id=1, source_target_pairs={{0,4},{1,5},{2,6},{3,7},{4,0},{5,1},{6,2},{7,3},{8,12},{9,13},{10,... | collective-permute-start | bytes 393224 | tf_op jit(solution)/shard_map/ppermute | solution.py:246
  34.6 13.1 %collective-permute-start.9 = (f32[2,128,128]{2,1,0:T(8,128)S(1)}, f32[2,128,128]{2,1,0:T(8,128)S(1)}, u32[]{:S(2)}, u32[]{:S(2)}) collective-permute-start(f32[2,128,128]{2,1,0:T(8,128)S(1)} %get-tuple-element.42), channel_id=1, source_target_pairs={{0,6},{1,7},{2,4},{3,5},{4,2},{5,3},{6,0},{7,1},{8,14},{9,15},{10,... | collective-permute-start | bytes 393224 | tf_op jit(solution)/shard_map/ppermute | solution.py:246
  38.8 11.4 %collective-permute-start.15 = (f32[392,128]{1,0:T(8,128)S(1)}, f32[392,128]{1,0:T(8,128)S(1)}, u32[]{:S(2)}, u32[]{:S(2)}) collective-permute-start(f32[392,128]{1,0:T(8,128)S(1)} %get-tuple-element.51), channel_id=1, source_target_pairs={{0,1},{1,0},{2,3},{3,2},{4,5},{5,4},{6,7},{7,6},{8,9},{9,8},{10,11... | collective-permute-start | bytes 602120 | tf_op jit(solution)/shard_map/ppermute | solution.py:246
  47.7 8.5 %collective-permute-start.10 = (f32[4,128,128]{2,1,0:T(8,128)S(1)}, f32[4,128,128]{2,1,0:T(8,128)S(1)}, u32[]{:S(2)}, u32[]{:S(2)}) collective-permute-start(f32[4,128,128]{2,1,0:T(8,128)S(1)} %get-tuple-element.44), channel_id=1, source_target_pairs={{0,1},{1,0},{2,3},{3,2},{4,5},{5,4},{6,7},{7,6},{8,9},{9,8},{10,11... | collective-permute-start | bytes 786440 | tf_op jit(solution)/shard_map/ppermute | solution.py:246
  47.8 8.4 %collective-permute-start.18 = (f32[264,128]{1,0:T(8,128)S(1)}, f32[264,128]{1,0:T(8,128)S(1)}, u32[]{:S(2)}, u32[]{:S(2)}) collective-permute-start(f32[264,128]{1,0:T(8,128)S(1)} %get-tuple-element.55), channel_id=1, source_target_pairs={{0,6},{1,7},{2,4},{3,5},{4,2},{5,3},{6,0},{7,1},{8,14},{9,15},{10,... | collective-permute-start | bytes 405512 | tf_op jit(solution)/shard_map/ppermute | solution.py:246
  50.2 8.4 %collective-permute-start.16 = (f32[264,128]{1,0:T(8,128)S(1)}, f32[264,128]{1,0:T(8,128)S(1)}, u32[]{:S(2)}, u32[]{:S(2)}) collective-permute-start(f32[264,128]{1,0:T(8,128)S(1)} %get-tuple-element.53), channel_id=1, source_target_pairs={{0,2},{1,3},{2,0},{3,1},{4,6},{5,7},{6,4},{7,5},{8,10},{9,11},{10,... | collective-permute-start | bytes 405512 | tf_op jit(solution)/shard_map/ppermute | solution.py:246
  51.8 12.4 %collective-permute-start.17 = (f32[264,128]{1,0:T(8,128)S(1)}, f32[264,128]{1,0:T(8,128)S(1)}, u32[]{:S(2)}, u32[]{:S(2)}) collective-permute-start(f32[264,128]{1,0:T(8,128)S(1)} %get-tuple-element.54), channel_id=1, source_target_pairs={{0,4},{1,5},{2,6},{3,7},{4,0},{5,1},{6,2},{7,3},{8,12},{9,13},{10,... | collective-permute-start | bytes 405512 | tf_op jit(solution)/shard_map/ppermute | solution.py:246
  56.2 1.3 %collective-permute-start.19 = (f32[136,128]{1,0:T(8,128)S(1)}, f32[136,128]{1,0:T(8,128)S(1)}, u32[]{:S(2)}, u32[]{:S(2)}) collective-permute-start(f32[136,128]{1,0:T(8,128)S(1)} %get-tuple-element.57), channel_id=1, source_target_pairs={{0,1},{1,0},{2,3},{3,2},{4,5},{5,4},{6,7},{7,6},{8,9},{9,8},{10,11... | collective-permute-start | bytes 208904 | tf_op jit(solution)/shard_map/ppermute | solution.py:246

commit v3 on v2

--- a/solution.py
+++ b/solution.py
@@ -17,7 +17,14 @@
 EXTRA = 8
 STEPS = 4
 OUT_STEPS = 8
+IN_WAYS = (0, 0)
+OUT_WAYS = (0, 1)
 VMEM_LIMIT = 12 * 2**20
+
+
+def device_at(me, step, near, lines, way):
+    line = (me // 2) ^ step if way == 0 else (me // 2 + way * step) & (lines - 1)
+    return 2 * line + ((me % 2) ^ near)
 
 
 def split(value):
@@ -25,7 +32,7 @@
     return high, (value - high.astype(F32)).astype(BF16)
 
 
-def pack_kernel(steps, x_ref, *refs):
+def pack_kernel(steps, way, x_ref, *refs):
     me = lax.axis_index("amp")
     out_refs, held, sems = refs[:-2], refs[-2], refs[-1]
     register, middle, lanes = held.shape
@@ -40,17 +47,17 @@
         copies[at].wait()
         for far, out in enumerate(out_refs):
             for near in range(2):
-                first = at * step * middle + (me ^ (2 * far + near))
+                first = at * step * middle + device_at(me, far, near, len(out_refs), way)
                 out[near, at * step : (at + 1) * step, :] = rows[pl.ds(first, step, stride=middle), :]
 
 
-def pack_both_kernel(x_ref, side_ref, *out_refs):
+def pack_both_kernel(way, x_ref, side_ref, *out_refs):
     me = lax.axis_index("amp")
     register, middle, lanes = x_ref.shape
     for near, ref in enumerate((x_ref, side_ref)):
         rows = ref.reshape(register * middle, lanes)
         for far, out in enumerate(out_refs):
-            out[near] = rows[pl.ds(me ^ (2 * far), register, stride=middle), :]
+            out[near] = rows[pl.ds(device_at(me, far, 0, len(out_refs), way), register, stride=middle), :]
 
 
 def part_kernel(*refs):
@@ -143,7 +150,11 @@
     return refs[near].at[far] if len(refs) == 2 else refs[far].at[near]
 
 
-def sections_kernel(sections, lines, pieces, last, *refs):
+def later_turns(lines):
+    return [turn for turn in range(lines) if turn != 1]
+
+
+def sections_kernel(sections, lines, ways, pieces, last, *refs):
     amp = 2 * lines
     piece_refs, (low_ref, high_ref) = refs[:pieces], refs[pieces : pieces + 2]
     at = pieces + 2
@@ -162,7 +173,7 @@
         for near in range(2):
             value = piece_of(piece_refs, far, near)[...]
             total = squares(total, value)
-            x[me ^ (2 * far + near)] = value
+            x[device_at(me, far, near, lines, -ways[0])] = value
     sums = [total]
     for section in range(sections):
         low, high = low_ref[section], high_ref[section]
@@ -187,26 +198,26 @@
     if not last:
         for far in range(lines):
             for near in range(2):
-                out_refs[far][near] = x[me ^ (2 * far + near)]
+                out_refs[far][near] = x[device_at(me, far, near, lines, ways[1])]
         out_refs[lines][...] = rows
         return
     rows = rows + sums_in[...]
     first = out_refs[0]
     for near in range(2):
-        first[near * register : (near + 1) * register, :] = x[me ^ (2 * (lines - 1) + near)]
-        for far in range(lines - 1):
-            out_refs[1 + near][far * register : (far + 1) * register, :] = x[me ^ (2 * far + near)]
+        first[near * register : (near + 1) * register, :] = x[device_at(me, 1, near, lines, ways[1])]
+        for at, far in enumerate(later_turns(lines)):
+            out_refs[1 + near][at * register : (at + 1) * register, :] = x[device_at(me, far, near, lines, ways[1])]
         out_refs[1 + near][(lines - 1) * register :, :] = rows
     first[2 * register :, :] = rows
 
 
-def unpack_kernel(lines, early, steps, total_amps, *refs):
+def unpack_kernel(lines, ways, early, steps, total_amps, *refs):
     held, refs = refs[: 2 * early], refs[2 * early :]
-    joined, far_refs, (x_ref, logs_ref, out, logs_held, sems) = refs[: lines - 1], refs[lines - 1 : lines + 1], refs[lines + 1 :]
+    joined, first_refs, (x_ref, logs_ref, out, logs_held, sems) = refs[: lines - 1], refs[lines - 1 : lines + 1], refs[lines + 1 :]
     me = lax.axis_index("amp")
     register, middle, lanes = out.shape
     sections = logs_ref.shape[1]
-    totals = far_refs[0][register:, :] + far_refs[1][register:, :]
+    totals = first_refs[0][register:, :] + first_refs[1][register:, :]
     for ref in joined:
         totals = totals + ref[2 * register :, :]
     totals = jnp.sum(totals, axis=1, keepdims=True)
@@ -221,11 +232,13 @@
                 for near in range(2):
                     if chunk < early:
                         value = held[2 * chunk + near][far, low:high, :]
-                    elif far < lines - 1:
-                        value = joined[far][near * register + low : near * register + high, :]
                     else:
-                        value = far_refs[near][low:high, :]
-                    m = chunk * 2 * lines + (me ^ (2 * far + near))
+                        if far == 1:
+                            value = first_refs[near][low:high, :]
+                        else:
+                            at_turn = later_turns(lines).index(far)
+                            value = joined[at_turn][near * register + low : near * register + high, :]
+                    m = chunk * 2 * lines + device_at(me, far, near, lines, -ways[chunk])
                     flat[pl.ds(low * middle + m, step, stride=middle), :] = value * scale
         span = pl.ds(low, step)
         copies.append(pltpu.make_async_copy(out.at[span], x_ref.at[span], sems.at[at]))
@@ -246,12 +259,20 @@
     return lax.ppermute(piece, axis, [(i, i ^ k) for i in range(size)])
 
 
+def shift(piece, step, lines, way):
+    if step == 0:
+        return piece
+    pairs = [(me, device_at(me, step, 0, lines, way)) for me in range(2 * lines)]
+    return lax.ppermute(piece, "amp", pairs)
+
+
 def body_fast(states, gate_blocks, kraus_picks, block_targets):
     amp_local = states.shape[1]
     register = gate_blocks.shape[-1]
     amp, sections = lax.axis_size("amp"), lax.axis_size("segment")
     middle = amp_local // (register * register)
     chunks, lines = middle // amp, amp // 2
+    in_ways, out_ways = [IN_WAYS[chunk > 0] for chunk in range(chunks)], [OUT_WAYS[chunk == chunks - 1] for chunk in range(chunks)]
     params = pltpu.CompilerParams(vmem_limit_bytes=VMEM_LIMIT)
 
     def array(*shape, dtype=F32):
@@ -261,10 +282,8 @@
         specs = dict(in_specs=[VMEM] * len(operands), out_specs=[VMEM] * len(out_shape))
         return pl.pallas_call(body, out_shape=out_shape, compiler_params=params, **{**specs, **options})(*operands)
 
-    def along(pieces):
-        count = len(pieces)
-        back = {far: swap(pieces[far], 2 * far, amp, "amp") for far in range(count - 1, -1, -1)}
-        return [back[far] for far in range(count)]
+    def along(pieces, way):
+        return [shift(piece, step, lines, way) for step, piece in enumerate(pieces)]
 
     def across(piece):
         return swap(piece, 1, amp, "amp")
@@ -275,18 +294,18 @@
     for chunk in range(chunks):
         if chunk == 0:
             packed = kernel(
-                functools.partial(pack_kernel, STEPS),
+                functools.partial(pack_kernel, STEPS, in_ways[0]),
                 pairs,
                 pltpu.with_memory_space_constraint(x, pltpu.HBM),
                 in_specs=[pl.BlockSpec(memory_space=pltpu.HBM)],
                 scratch_shapes=[pltpu.VMEM((register, amp, register), F32), pltpu.SemaphoreType.DMA((STEPS,))],
             )
-            near, other = kernel(part_kernel, halves, *along(packed))
+            near, other = kernel(part_kernel, halves, *along(packed, in_ways[0]))
             arrived.append([near, across(other)])
         else:
             own = x[:, chunk * amp : (chunk + 1) * amp, :]
-            packed = kernel(pack_both_kernel, pairs, own, across(own))
-            arrived.append(along(packed))
+            packed = kernel(functools.partial(pack_both_kernel, in_ways[chunk]), pairs, own, across(own))
+            arrived.append(along(packed, in_ways[chunk]))
 
     gates = [swap(gate_blocks[0], k, sections, "segment") for k in range(sections)]
     low, high = kernel(
@@ -304,7 +323,7 @@
         both = 2 * register + EXTRA
         aside = array((lines - 1) * register + EXTRA, register)
         results = kernel(
-            functools.partial(sections_kernel, sections, lines, len(pieces), last),
+            functools.partial(sections_kernel, sections, lines, (in_ways[chunk], out_ways[chunk]), len(pieces), last),
             [array(both, register), aside, aside] if last else pairs + [array(EXTRA, register)],
             *pieces,
             low,
@@ -314,19 +333,20 @@
         )
         if last:
             first, own, other = results
-            first = swap(first, 2 * (lines - 1), amp, "amp")
+            first = shift(first, 1, lines, out_ways[chunk])
             tall = [array(both, register)] * (lines - 1)
-            held += along(kernel(join_kernel, tall, own, across(other)))
+            joined = kernel(join_kernel, tall, own, across(other))
+            held += [shift(piece, k, lines, out_ways[chunk]) for k, piece in zip(later_turns(lines), joined)]
             tall = [array(register + EXTRA, register)] * 2
             near, other = kernel(part_last_kernel, tall, first)
             held += [near, across(other)]
         else:
             carried = [results[lines]]
-            near, other = kernel(part_kernel, halves, *along(results[:lines]))
+            near, other = kernel(part_kernel, halves, *along(results[:lines], out_ways[chunk]))
             held += [near, across(other)]
 
     out, logs = kernel(
-        functools.partial(unpack_kernel, lines, chunks - 1, OUT_STEPS, float(amp_local * amp)),
+        functools.partial(unpack_kernel, lines, out_ways, chunks - 1, OUT_STEPS, float(amp_local * amp)),
         [array(register, middle, register), array(1, sections)],
         *held,
         out_specs=[pl.BlockSpec(memory_space=pltpu.HBM)] * 2,

time: 65.6 us -> 63.4 us (0.966)
  waiting for transfers between devices: 27.4 us -> 22.8 us
  starting transfers between devices: 26.6 us -> 28.4 us
    ppermute x20 -> x8, waiting for transfers between devices: 27.4 us -> 1.64 us  [swap(): return lax.ppermute(piece, axis, [(i, i ^ k) for i in range(size)])]
    ppermute x0 -> x12, starting transfers between devices: none -> 21.6 us  [shift(): return lax.ppermute(piece, 'amp', pairs)]
    ppermute x0 -> x12, waiting for transfers between devices: none -> 21.2 us  [shift(): return lax.ppermute(piece, 'amp', pairs)]
    ppermute x20 -> x8, starting transfers between devices: 26.6 us -> 6.8 us  [swap(): return lax.ppermute(piece, axis, [(i, i ^ k) for i in range(size)])]
  transfers between devices with their start and end apart: 20 -> 20, of which waited for: 10 -> 9; matrix products, arithmetic and copies ran while one was open for 0% -> 0% of each run, Pallas kernels for 12% -> 13%
where the time goes in v3:
time: 63.4 us; the launch traced here: 62.6 us
  starting transfers between devices  28.4 us (45%)
  waiting for transfers between devices  22.8 us (36%)
  Pallas kernels  9.22 us (15%)
  local copies, waits for them, and re-layouts  1.39 us (2%)
  between operations  0.77 us (1%)
    ppermute x12, starting transfers between devices, shift(): return lax.ppermute(piece, 'amp', pairs)  21.6 us
    ppermute x12, waiting for transfers between devices, shift(): return lax.ppermute(piece, 'amp', pairs)  21.2 us
    pallas_call x10, Pallas kernels, kernel(): pl.pallas_call(body, out_shape=out_shape, compiler_params=params, **{**sp...  9.22 us
    ppermute x8, starting transfers between devices, swap(): return lax.ppermute(piece, axis, [(i, i ^ k) for i in range(size)])  6.8 us
    ppermute x8, waiting for transfers between devices, swap(): return lax.ppermute(piece, axis, [(i, i ^ k) for i in range(size)])  1.64 us
  transfers between devices with their start and end apart: 20, of which 9 were waited for; matrix products, arithmetic and copies ran while one was open for 0% of the time, Pallas kernels for 13%

profile of v3, /device:TPU:0, one launch (start us, length us, event | category | flops | bytes accessed | tf_op | source)
XLA Modules:
  0.0 62.6 jit_solution(7915723124583678591)
XLA Ops:
  0.6 1.1 %slice.4.x_ref = f32[128,8,128]{2,1,0:T(8,128)S(1)} slice(f32[128,16,128]{2,1,0:T(8,128)} %bitcast.8), slice={[0:128], [8:16], [0:128]} | slice | bytes 1048576 | tf_op jit(solution)/shard_map/slice | solution.py:306
  2.3 1.2 %shard_map.59 = (f32[2,128,128]{2,1,0:T(8,128)S(1)}, f32[2,128,128]{2,1,0:T(8,128)S(1)}, f32[2,128,128]{2,1,0:T(8,128)S(1)}, f32[2,128,128]{2,1,0:T(8,128)S(1)}) custom-call(f32[128,16,128]{2,1,0:T(8,128)} %bitcast.9), custom_call_target="tpu_custom_call" | custom-call | tf_op jit(solution)/shard_map/pallas_call | solution.py:283
  3.5 2.7 %collective-permute-start = (f32[2,128,128]{2,1,0:T(8,128)S(1)}, f32[2,128,128]{2,1,0:T(8,128)S(1)}, u32[]{:S(2)}, u32[]{:S(2)}) collective-permute-start(f32[2,128,128]{2,1,0:T(8,128)S(1)} %get-tuple-element.32), channel_id=1, source_target_pairs={{0,2},{1,3},{2,0},{3,1},{4,6},{5,7},{6,4},{7,5},{8,10},{9,11},{10,... | collective-permute-start | bytes 393224 | tf_op jit(solution)/shard_map/ppermute | solution.py:266
  6.1 2.6 %collective-permute-start.1 = (f32[2,128,128]{2,1,0:T(8,128)S(1)}, f32[2,128,128]{2,1,0:T(8,128)S(1)}, u32[]{:S(2)}, u32[]{:S(2)}) collective-permute-start(f32[2,128,128]{2,1,0:T(8,128)S(1)} %get-tuple-element.33), channel_id=1, source_target_pairs={{0,4},{1,5},{2,6},{3,7},{4,0},{5,1},{6,2},{7,3},{8,12},{9,13},{10,... | collective-permute-start | bytes 393224 | tf_op jit(solution)/shard_map/ppermute | solution.py:266
  8.7 2.7 %collective-permute-start.6 = (f32[3,128,128]{2,1,0:T(8,128)S(1)}, f32[3,128,128]{2,1,0:T(8,128)S(1)}, u32[]{:S(2)}, u32[]{:S(2)}) collective-permute-start(f32[3,128,128]{2,1,0:T(8,128)S(1)} %bitcast.4), channel_id=1, source_target_pairs={{0,24},{8,16},{16,8},{24,0},{1,25},{9,17},{17,9},{25,1},{2,26},{10... | collective-permute-start | bytes 589832 | tf_op jit(solution)/shard_map/ppermute | solution.py:259
  12.4 1.7 %collective-permute-start.5 = (f32[3,128,128]{2,1,0:T(8,128)S(1)}, f32[3,128,128]{2,1,0:T(8,128)S(1)}, u32[]{:S(2)}, u32[]{:S(2)}) collective-permute-start(f32[3,128,128]{2,1,0:T(8,128)S(1)} %bitcast.5), channel_id=1, source_target_pairs={{0,16},{8,24},{16,0},{24,8},{1,17},{9,25},{17,1},{25,9},{2,18},{10... | collective-permute-start | bytes 589832 | tf_op jit(solution)/shard_map/ppermute | solution.py:259
  14.2 4.9 %collective-permute-done.1.refs_2_ = f32[2,128,128]{2,1,0:T(8,128)S(1)} collective-permute-done((f32[2,128,128]{2,1,0:T(8,128)S(1)}, f32[2,128,128]{2,1,0:T(8,128)S(1)}, u32[]{:S(2)}, u32[]{:S(2)}) %collective-permute-start.1) | collective-permute-done | bytes 131104 | tf_op jit(solution)/shard_map/ppermute | solution.py:266
  19.2 1.6 %collective-permute-start.4 = (f32[3,128,128]{2,1,0:T(8,128)S(1)}, f32[3,128,128]{2,1,0:T(8,128)S(1)}, u32[]{:S(2)}, u32[]{:S(2)}) collective-permute-start(f32[3,128,128]{2,1,0:T(8,128)S(1)} %bitcast.6), channel_id=1, source_target_pairs={{0,8},{8,0},{16,24},{24,16},{1,9},{9,1},{17,25},{25,17},{2,10},{10... | collective-permute-start | bytes 589832 | tf_op jit(solution)/shard_map/ppermute | solution.py:259
  20.9 2.6 %collective-permute-start.12 = (f32[2,128,128]{2,1,0:T(8,128)S(1)}, f32[2,128,128]{2,1,0:T(8,128)S(1)}, u32[]{:S(2)}, u32[]{:S(2)}) collective-permute-start(f32[2,128,128]{2,1,0:T(8,128)S(1)} %get-tuple-element.46), channel_id=1, source_target_pairs={{0,2},{1,3},{2,0},{3,1},{4,6},{5,7},{6,4},{7,5},{8,10},{9,11},{10,... | collective-permute-start | bytes 393224 | tf_op jit(solution)/shard_map/ppermute | solution.py:266
  23.5 1.1 %collective-permute-start.13 = (f32[2,128,128]{2,1,0:T(8,128)S(1)}, f32[2,128,128]{2,1,0:T(8,128)S(1)}, u32[]{:S(2)}, u32[]{:S(2)}) collective-permute-start(f32[2,128,128]{2,1,0:T(8,128)S(1)} %get-tuple-element.47), channel_id=1, source_target_pairs={{0,4},{1,5},{2,6},{3,7},{4,0},{5,1},{6,2},{7,3},{8,12},{9,13},{10,... | collective-permute-start | bytes 393224 | tf_op jit(solution)/shard_map/ppermute | solution.py:266
  24.6 1.4 %collective-permute-start.14 = (f32[2,128,128]{2,1,0:T(8,128)S(1)}, f32[2,128,128]{2,1,0:T(8,128)S(1)}, u32[]{:S(2)}, u32[]{:S(2)}) collective-permute-start(f32[2,128,128]{2,1,0:T(8,128)S(1)} %get-tuple-element.48), channel_id=1, source_target_pairs={{0,6},{1,7},{2,4},{3,5},{4,2},{5,3},{6,0},{7,1},{8,14},{9,15},{10,... | collective-permute-start | bytes 393224 | tf_op jit(solution)/shard_map/ppermute | solution.py:266
  26.8 2.0 %shard_map.61 = (bf16[4,256,256]{2,1,0:T(8,128)(2,1)S(1)}, bf16[4,256,256]{2,1,0:T(8,128)(2,1)S(1)}) custom-call(s32[4,3,7]{2,1,0:T(4,128)S(1)} %copy.6.picks_ref, s32[4,3]{1,0:T(4,128)S(1)} %copy-done.1, f32[3,128,128]{2,1,0:T(8,128)S(1)} %bitcast.7, f32[3,128,128]{2,1,0:T(8,128)S(1)} %collective-permute-done.4.refs_1_, ...), custom_call_target="tpu_custom_call" | custom-call | tf_op jit(solution)/shard_map/pallas_call | solution.py:283
  28.8 2.3 %shard_map.62 = (f32[2,128,128]{2,1,0:T(8,128)S(1)}, f32[2,128,128]{2,1,0:T(8,128)S(1)}, f32[2,128,128]{2,1,0:T(8,128)S(1)}, f32[2,128,128]{2,1,0:T(8,128)S(1)}, f32[8,128]{1,0:T(8,128)S(1)}) custom-call(f32[4,128,128]{2,1,0:T(8,128)S(1)} %get-tuple-element.35.refs_0_, f32[4,128,128]{2,1,0:T(8,128)S(1)} %collective-permute-done.3.refs_1_, ...), custom_call_target="tpu_custom_call" | custom-call | tf_op jit(solution)/shard_map/pallas_call | solution.py:283
  31.1 2.4 %collective-permute-start.7 = (f32[2,128,128]{2,1,0:T(8,128)S(1)}, f32[2,128,128]{2,1,0:T(8,128)S(1)}, u32[]{:S(2)}, u32[]{:S(2)}) collective-permute-start(f32[2,128,128]{2,1,0:T(8,128)S(1)} %get-tuple-element.40), channel_id=1, source_target_pairs={{0,2},{1,3},{2,0},{3,1},{4,6},{5,7},{6,4},{7,5},{8,10},{9,11},{10,... | collective-permute-start | bytes 393224 | tf_op jit(solution)/shard_map/ppermute | solution.py:266
  33.5 1.1 %collective-permute-start.8 = (f32[2,128,128]{2,1,0:T(8,128)S(1)}, f32[2,128,128]{2,1,0:T(8,128)S(1)}, u32[]{:S(2)}, u32[]{:S(2)}) collective-permute-start(f32[2,128,128]{2,1,0:T(8,128)S(1)} %get-tuple-element.41), channel_id=1, source_target_pairs={{0,4},{1,5},{2,6},{3,7},{4,0},{5,1},{6,2},{7,3},{8,12},{9,13},{10,... | collective-permute-start | bytes 393224 | tf_op jit(solution)/shard_map/ppermute | solution.py:266
  34.6 1.4 %collective-permute-start.9 = (f32[2,128,128]{2,1,0:T(8,128)S(1)}, f32[2,128,128]{2,1,0:T(8,128)S(1)}, u32[]{:S(2)}, u32[]{:S(2)}) collective-permute-start(f32[2,128,128]{2,1,0:T(8,128)S(1)} %get-tuple-element.42), channel_id=1, source_target_pairs={{0,6},{1,7},{2,4},{3,5},{4,2},{5,3},{6,0},{7,1},{8,14},{9,15},{10,... | collective-permute-start | bytes 393224 | tf_op jit(solution)/shard_map/ppermute | solution.py:266
  36.4 2.3 %shard_map.65 = (f32[264,128]{1,0:T(8,128)S(1)}, f32[392,128]{1,0:T(8,128)S(1)}, f32[392,128]{1,0:T(8,128)S(1)}) custom-call(f32[2,128,128]{2,1,0:T(8,128)S(1)} %get-tuple-element.45.refs_0_, f32[2,128,128]{2,1,0:T(8,128)S(1)} %collective-permute-done.12.refs_1_, f32[2,128,128]{2,1,0:T(8,128)S(1)} %collective-permute-done.13.refs_2_, ...), custom_call_target="tpu_custom_call" | custom-call | tf_op jit(solution)/shard_map/pallas_call | solution.py:283
  39.3 8.4 %collective-permute-done.8.refs_2_ = f32[2,128,128]{2,1,0:T(8,128)S(1)} collective-permute-done((f32[2,128,128]{2,1,0:T(8,128)S(1)}, f32[2,128,128]{2,1,0:T(8,128)S(1)}, u32[]{:S(2)}, u32[]{:S(2)}) %collective-permute-start.8) | collective-permute-done | bytes 131104 | tf_op jit(solution)/shard_map/ppermute | solution.py:266
  47.8 2.4 %collective-permute-start.18 = (f32[264,128]{1,0:T(8,128)S(1)}, f32[264,128]{1,0:T(8,128)S(1)}, u32[]{:S(2)}, u32[]{:S(2)}) collective-permute-start(f32[264,128]{1,0:T(8,128)S(1)} %get-tuple-element.55), channel_id=1, source_target_pairs={{0,2},{1,3},{2,4},{3,5},{4,6},{5,7},{6,0},{7,1},{8,10},{9,11},{10,... | collective-permute-start | bytes 405512 | tf_op jit(solution)/shard_map/ppermute | solution.py:266
  51.2 2.9 %collective-permute-start.17 = (f32[264,128]{1,0:T(8,128)S(1)}, f32[264,128]{1,0:T(8,128)S(1)}, u32[]{:S(2)}, u32[]{:S(2)}) collective-permute-start(f32[264,128]{1,0:T(8,128)S(1)} %get-tuple-element.54), channel_id=1, source_target_pairs={{0,6},{1,7},{2,0},{3,1},{4,2},{5,3},{6,4},{7,5},{8,14},{9,15},{10,... | collective-permute-start | bytes 405512 | tf_op jit(solution)/shard_map/ppermute | solution.py:266
  54.1 2.0 %collective-permute-done.18.piece_ref = f32[264,128]{1,0:T(8,128)S(1)} collective-permute-done((f32[264,128]{1,0:T(8,128)S(1)}, f32[264,128]{1,0:T(8,128)S(1)}, u32[]{:S(2)}, u32[]{:S(2)}) %collective-permute-start.18) | collective-permute-done | bytes 135200 | tf_op jit(solution)/shard_map/ppermute | solution.py:266
  56.3 1.2 %collective-permute-done.19.refs_6_ = f32[136,128]{1,0:T(8,128)S(1)} collective-permute-done((f32[136,128]{1,0:T(8,128)S(1)}, f32[136,128]{1,0:T(8,128)S(1)}, u32[]{:S(2)}, u32[]{:S(2)}) %collective-permute-start.19) | collective-permute-done | bytes 69664 | tf_op jit(solution)/shard_map/ppermute | solution.py:259
  57.5 3.9 %collective-permute-done.16.refs_3_ = f32[264,128]{1,0:T(8,128)S(1)} collective-permute-done((f32[264,128]{1,0:T(8,128)S(1)}, f32[264,128]{1,0:T(8,128)S(1)}, u32[]{:S(2)}, u32[]{:S(2)}) %collective-permute-start.16) | collective-permute-done | bytes 135200 | tf_op jit(solution)/shard_map/ppermute | solution.py:266
  61.4 1.2 %shard_map.68 = (f32[128,16,128]{2,1,0:T(8,128)}, f32[1,4]{1,0:T(1,128)}) custom-call(f32[4,128,128]{2,1,0:T(8,128)S(1)} %get-tuple-element.43.refs_0_, f32[4,128,128]{2,1,0:T(8,128)S(1)} %collective-permute-done.10.refs_1_, f32[264,128]{1,0:T(8,128)S(1)} %get-tuple-element.52.refs_2_, f32[264,128]{1,0:T(8,128)S(1)} %collective-permute-done.16.refs_3_, ...), custom_call_target="tpu_custom_call" | custom-call | tf_op jit(solution)/shard_map/pallas_call | solution.py:283
  (34 shorter events, 4.8 us)
Async XLA Ops:
  1.7 7.0 %copy-start = (f32[1,3,128,128]{3,2,1,0:T(8,128)S(1)}, f32[1,3,128,128]{3,2,1,0:T(8,128)}, u32[]{:S(2)}) copy-start(f32[1,3,128,128]{3,2,1,0:T(8,128)} %param.5) | copy-start | bytes 589828
  1.7 19.0 %collective-permute-start.11 = (f32[128,8,128]{2,1,0:T(8,128)S(1)}, f32[128,8,128]{2,1,0:T(8,128)S(1)}, u32[]{:S(2)}, u32[]{:S(2)}) collective-permute-start(f32[128,8,128]{2,1,0:T(8,128)S(1)} %slice.4.x_ref), channel_id=1, source_target_pairs={{0,1},{1,0},{2,3},{3,2},{4,5},{5,4},{6,7},{7,6},{8,9},{9,8},{10,11... | collective-permute-start | bytes 1572872 | tf_op jit(solution)/shard_map/ppermute | solution.py:259
  3.5 9.0 %collective-permute-start = (f32[2,128,128]{2,1,0:T(8,128)S(1)}, f32[2,128,128]{2,1,0:T(8,128)S(1)}, u32[]{:S(2)}, u32[]{:S(2)}) collective-permute-start(f32[2,128,128]{2,1,0:T(8,128)S(1)} %get-tuple-element.32), channel_id=1, source_target_pairs={{0,2},{1,3},{2,0},{3,1},{4,6},{5,7},{6,4},{7,5},{8,10},{9,11},{10,... | collective-permute-start | bytes 393224 | tf_op jit(solution)/shard_map/ppermute | solution.py:266
  6.1 12.9 %collective-permute-start.1 = (f32[2,128,128]{2,1,0:T(8,128)S(1)}, f32[2,128,128]{2,1,0:T(8,128)S(1)}, u32[]{:S(2)}, u32[]{:S(2)}) collective-permute-start(f32[2,128,128]{2,1,0:T(8,128)S(1)} %get-tuple-element.33), channel_id=1, source_target_pairs={{0,4},{1,5},{2,6},{3,7},{4,0},{5,1},{6,2},{7,3},{8,12},{9,13},{10,... | collective-permute-start | bytes 393224 | tf_op jit(solution)/shard_map/ppermute | solution.py:266
  8.7 10.3 %collective-permute-start.2 = (f32[2,128,128]{2,1,0:T(8,128)S(1)}, f32[2,128,128]{2,1,0:T(8,128)S(1)}, u32[]{:S(2)}, u32[]{:S(2)}) collective-permute-start(f32[2,128,128]{2,1,0:T(8,128)S(1)} %get-tuple-element.34), channel_id=1, source_target_pairs={{0,6},{1,7},{2,4},{3,5},{4,2},{5,3},{6,0},{7,1},{8,14},{9,15},{10,... | collective-permute-start | bytes 393224 | tf_op jit(solution)/shard_map/ppermute | solution.py:266
  8.7 14.8 %collective-permute-start.6 = (f32[3,128,128]{2,1,0:T(8,128)S(1)}, f32[3,128,128]{2,1,0:T(8,128)S(1)}, u32[]{:S(2)}, u32[]{:S(2)}) collective-permute-start(f32[3,128,128]{2,1,0:T(8,128)S(1)} %bitcast.4), channel_id=1, source_target_pairs={{0,24},{8,16},{16,8},{24,0},{1,25},{9,17},{17,9},{25,1},{2,26},{10... | collective-permute-start | bytes 589832 | tf_op jit(solution)/shard_map/ppermute | solution.py:259
  12.4 12.2 %collective-permute-start.5 = (f32[3,128,128]{2,1,0:T(8,128)S(1)}, f32[3,128,128]{2,1,0:T(8,128)S(1)}, u32[]{:S(2)}, u32[]{:S(2)}) collective-permute-start(f32[3,128,128]{2,1,0:T(8,128)S(1)} %bitcast.5), channel_id=1, source_target_pairs={{0,16},{8,24},{16,0},{24,8},{1,17},{9,25},{17,1},{25,9},{2,18},{10... | collective-permute-start | bytes 589832 | tf_op jit(solution)/shard_map/ppermute | solution.py:259
  19.1 9.7 %collective-permute-start.3 = (f32[4,128,128]{2,1,0:T(8,128)S(1)}, f32[4,128,128]{2,1,0:T(8,128)S(1)}, u32[]{:S(2)}, u32[]{:S(2)}) collective-permute-start(f32[4,128,128]{2,1,0:T(8,128)S(1)} %get-tuple-element.36), channel_id=1, source_target_pairs={{0,1},{1,0},{2,3},{3,2},{4,5},{5,4},{6,7},{7,6},{8,9},{9,8},{10,11... | collective-permute-start | bytes 786440 | tf_op jit(solution)/shard_map/ppermute | solution.py:259
  19.2 7.3 %collective-permute-start.4 = (f32[3,128,128]{2,1,0:T(8,128)S(1)}, f32[3,128,128]{2,1,0:T(8,128)S(1)}, u32[]{:S(2)}, u32[]{:S(2)}) collective-permute-start(f32[3,128,128]{2,1,0:T(8,128)S(1)} %bitcast.6), channel_id=1, source_target_pairs={{0,8},{8,0},{16,24},{24,16},{1,9},{9,1},{17,25},{25,17},{2,10},{10... | collective-permute-start | bytes 589832 | tf_op jit(solution)/shard_map/ppermute | solution.py:259
  20.9 5.2 %copy-start.2 = (s32[1,4,3,7]{3,1,2,0:T(4,128)S(1)}, s32[1,4,3,7]{3,1,2,0:T(4,128)}, u32[]{:S(2)}) copy-start(s32[1,4,3,7]{3,1,2,0:T(4,128)} %param.6) | copy-start | bytes 1012
  20.9 13.7 %collective-permute-start.12 = (f32[2,128,128]{2,1,0:T(8,128)S(1)}, f32[2,128,128]{2,1,0:T(8,128)S(1)}, u32[]{:S(2)}, u32[]{:S(2)}) collective-permute-start(f32[2,128,128]{2,1,0:T(8,128)S(1)} %get-tuple-element.46), channel_id=1, source_target_pairs={{0,2},{1,3},{2,0},{3,1},{4,6},{5,7},{6,4},{7,5},{8,10},{9,11},{10,... | collective-permute-start | bytes 393224 | tf_op jit(solution)/shard_map/ppermute | solution.py:266
  23.5 12.9 %collective-permute-start.13 = (f32[2,128,128]{2,1,0:T(8,128)S(1)}, f32[2,128,128]{2,1,0:T(8,128)S(1)}, u32[]{:S(2)}, u32[]{:S(2)}) collective-permute-start(f32[2,128,128]{2,1,0:T(8,128)S(1)} %get-tuple-element.47), channel_id=1, source_target_pairs={{0,4},{1,5},{2,6},{3,7},{4,0},{5,1},{6,2},{7,3},{8,12},{9,13},{10,... | collective-permute-start | bytes 393224 | tf_op jit(solution)/shard_map/ppermute | solution.py:266
  24.6 11.8 %collective-permute-start.14 = (f32[2,128,128]{2,1,0:T(8,128)S(1)}, f32[2,128,128]{2,1,0:T(8,128)S(1)}, u32[]{:S(2)}, u32[]{:S(2)}) collective-permute-start(f32[2,128,128]{2,1,0:T(8,128)S(1)} %get-tuple-element.48), channel_id=1, source_target_pairs={{0,6},{1,7},{2,4},{3,5},{4,2},{5,3},{6,0},{7,1},{8,14},{9,15},{10,... | collective-permute-start | bytes 393224 | tf_op jit(solution)/shard_map/ppermute | solution.py:266
  26.1 0.7 %copy-start.1 = (s32[4,3]{1,0:T(4,128)S(1)}, s32[4,3]{1,0:T(4,128)}, u32[]{:S(2)}) copy-start(s32[4,3]{1,0:T(4,128)} %targets_ref.1) | copy-start | bytes 148
  31.1 8.2 %collective-permute-start.7 = (f32[2,128,128]{2,1,0:T(8,128)S(1)}, f32[2,128,128]{2,1,0:T(8,128)S(1)}, u32[]{:S(2)}, u32[]{:S(2)}) collective-permute-start(f32[2,128,128]{2,1,0:T(8,128)S(1)} %get-tuple-element.40), channel_id=1, source_target_pairs={{0,2},{1,3},{2,0},{3,1},{4,6},{5,7},{6,4},{7,5},{8,10},{9,11},{10,... | collective-permute-start | bytes 393224 | tf_op jit(solution)/shard_map/ppermute | solution.py:266
  33.5 14.2 %collective-permute-start.8 = (f32[2,128,128]{2,1,0:T(8,128)S(1)}, f32[2,128,128]{2,1,0:T(8,128)S(1)}, u32[]{:S(2)}, u32[]{:S(2)}) collective-permute-start(f32[2,128,128]{2,1,0:T(8,128)S(1)} %get-tuple-element.41), channel_id=1, source_target_pairs={{0,4},{1,5},{2,6},{3,7},{4,0},{5,1},{6,2},{7,3},{8,12},{9,13},{10,... | collective-permute-start | bytes 393224 | tf_op jit(solution)/shard_map/ppermute | solution.py:266
  34.6 13.1 %collective-permute-start.9 = (f32[2,128,128]{2,1,0:T(8,128)S(1)}, f32[2,128,128]{2,1,0:T(8,128)S(1)}, u32[]{:S(2)}, u32[]{:S(2)}) collective-permute-start(f32[2,128,128]{2,1,0:T(8,128)S(1)} %get-tuple-element.42), channel_id=1, source_target_pairs={{0,6},{1,7},{2,4},{3,5},{4,2},{5,3},{6,0},{7,1},{8,14},{9,15},{10,... | collective-permute-start | bytes 393224 | tf_op jit(solution)/shard_map/ppermute | solution.py:266
  38.8 11.4 %collective-permute-start.15 = (f32[392,128]{1,0:T(8,128)S(1)}, f32[392,128]{1,0:T(8,128)S(1)}, u32[]{:S(2)}, u32[]{:S(2)}) collective-permute-start(f32[392,128]{1,0:T(8,128)S(1)} %get-tuple-element.51), channel_id=1, source_target_pairs={{0,1},{1,0},{2,3},{3,2},{4,5},{5,4},{6,7},{7,6},{8,9},{9,8},{10,11... | collective-permute-start | bytes 602120 | tf_op jit(solution)/shard_map/ppermute | solution.py:259
  47.7 8.6 %collective-permute-start.10 = (f32[4,128,128]{2,1,0:T(8,128)S(1)}, f32[4,128,128]{2,1,0:T(8,128)S(1)}, u32[]{:S(2)}, u32[]{:S(2)}) collective-permute-start(f32[4,128,128]{2,1,0:T(8,128)S(1)} %get-tuple-element.44), channel_id=1, source_target_pairs={{0,1},{1,0},{2,3},{3,2},{4,5},{5,4},{6,7},{7,6},{8,9},{9,8},{10,11... | collective-permute-start | bytes 786440 | tf_op jit(solution)/shard_map/ppermute | solution.py:259
  47.8 8.4 %collective-permute-start.18 = (f32[264,128]{1,0:T(8,128)S(1)}, f32[264,128]{1,0:T(8,128)S(1)}, u32[]{:S(2)}, u32[]{:S(2)}) collective-permute-start(f32[264,128]{1,0:T(8,128)S(1)} %get-tuple-element.55), channel_id=1, source_target_pairs={{0,2},{1,3},{2,4},{3,5},{4,6},{5,7},{6,0},{7,1},{8,10},{9,11},{10,... | collective-permute-start | bytes 405512 | tf_op jit(solution)/shard_map/ppermute | solution.py:266
  50.2 11.2 %collective-permute-start.16 = (f32[264,128]{1,0:T(8,128)S(1)}, f32[264,128]{1,0:T(8,128)S(1)}, u32[]{:S(2)}, u32[]{:S(2)}) collective-permute-start(f32[264,128]{1,0:T(8,128)S(1)} %get-tuple-element.53), channel_id=1, source_target_pairs={{0,4},{1,5},{2,6},{3,7},{4,0},{5,1},{6,2},{7,3},{8,12},{9,13},{10,... | collective-permute-start | bytes 405512 | tf_op jit(solution)/shard_map/ppermute | solution.py:266
  51.2 10.2 %collective-permute-start.17 = (f32[264,128]{1,0:T(8,128)S(1)}, f32[264,128]{1,0:T(8,128)S(1)}, u32[]{:S(2)}, u32[]{:S(2)}) collective-permute-start(f32[264,128]{1,0:T(8,128)S(1)} %get-tuple-element.54), channel_id=1, source_target_pairs={{0,6},{1,7},{2,0},{3,1},{4,2},{5,3},{6,4},{7,5},{8,14},{9,15},{10,... | collective-permute-start | bytes 405512 | tf_op jit(solution)/shard_map/ppermute | solution.py:266
  56.2 1.3 %collective-permute-start.19 = (f32[136,128]{1,0:T(8,128)S(1)}, f32[136,128]{1,0:T(8,128)S(1)}, u32[]{:S(2)}, u32[]{:S(2)}) collective-permute-start(f32[136,128]{1,0:T(8,128)S(1)} %get-tuple-element.57), channel_id=1, source_target_pairs={{0,1},{1,0},{2,3},{3,2},{4,5},{5,4},{6,7},{7,6},{8,9},{9,8},{10,11... | collective-permute-start | bytes 208904 | tf_op jit(solution)/shard_map/ppermute | solution.py:259

commit v4 on v3

--- a/solution.py
+++ b/solution.py
@@ -15,7 +15,6 @@
 VMEM = pl.BlockSpec(memory_space=pltpu.VMEM)
 SMEM = pl.BlockSpec(memory_space=pltpu.SMEM)
 EXTRA = 8
-STEPS = 4
 OUT_STEPS = 8
 IN_WAYS = (0, 0)
 OUT_WAYS = (0, 1)
@@ -32,23 +31,16 @@
     return high, (value - high.astype(F32)).astype(BF16)
 
 
-def pack_kernel(steps, way, x_ref, *refs):
+def take_kernel(steps, lines, way, pairs_ref, *refs):
     me = lax.axis_index("amp")
-    out_refs, held, sems = refs[:-2], refs[-2], refs[-1]
-    register, middle, lanes = held.shape
-    step = register // steps
+    out_refs, sems = refs[:-1], refs[-1]
     copies = []
-    for at in range(steps):
-        span = pl.ds(at * step, step)
-        copies.append(pltpu.make_async_copy(x_ref.at[span, 0:middle, :], held.at[span], sems.at[at]))
+    for at, (step, out) in enumerate(zip(steps, out_refs)):
+        pair = device_at(me, step, 0, lines, way) // 2
+        copies.append(pltpu.make_async_copy(pairs_ref.at[:, pair], out, sems.at[at]))
         copies[-1].start()
-    rows = held.reshape(register * middle, lanes)
-    for at in range(steps):
-        copies[at].wait()
-        for far, out in enumerate(out_refs):
-            for near in range(2):
-                first = at * step * middle + device_at(me, far, near, len(out_refs), way)
-                out[near, at * step : (at + 1) * step, :] = rows[pl.ds(first, step, stride=middle), :]
+    for copy in copies:
+        copy.wait()
 
 
 def pack_both_kernel(way, x_ref, side_ref, *out_refs):
@@ -65,6 +57,15 @@
     for far in range(lines):
         refs[lines][far] = refs[far][0]
         refs[lines + 1][far] = refs[far][1]
+
+
+def part_first_kernel(*refs):
+    lines = len(refs) - 2
+    south = lax.axis_index("amp") % 2 == 0
+    for far in range(lines):
+        values = refs[far][:, 0, :], refs[far][:, 1, :]
+        refs[lines][far] = jnp.where(south, values[0], values[1])
+        refs[lines + 1][far] = jnp.where(south, values[1], values[0])
 
 
 def part_last_kernel(piece_ref, near_ref, other_ref):
@@ -293,14 +294,19 @@
     arrived = []
     for chunk in range(chunks):
         if chunk == 0:
-            packed = kernel(
-                functools.partial(pack_kernel, STEPS, in_ways[0]),
-                pairs,
-                pltpu.with_memory_space_constraint(x, pltpu.HBM),
-                in_specs=[pl.BlockSpec(memory_space=pltpu.HBM)],
-                scratch_shapes=[pltpu.VMEM((register, amp, register), F32), pltpu.SemaphoreType.DMA((STEPS,))],
-            )
-            near, other = kernel(part_kernel, halves, *along(packed, in_ways[0]))
+            by_pairs = pltpu.with_memory_space_constraint(states.reshape(register, middle // 2, 2, register), pltpu.HBM)
+            packed = {}
+            for steps in ([lines - 1], list(range(lines - 1))):
+                taken = kernel(
+                    functools.partial(take_kernel, steps, lines, in_ways[0]),
+                    [array(register, 2, register)] * len(steps),
+                    by_pairs,
+                    in_specs=[pl.BlockSpec(memory_space=pltpu.HBM)],
+                    scratch_shapes=[pltpu.SemaphoreType.DMA((len(steps),))],
+                )
+                packed.update(zip(steps, taken))
+            pieces = along([packed[step] for step in range(lines)], in_ways[0])
+            near, other = kernel(part_first_kernel, halves, *pieces)
             arrived.append([near, across(other)])
         else:
             own = x[:, chunk * amp : (chunk + 1) * amp, :]

time: 63.4 us -> 61.9 us (0.976)
  waiting for transfers between devices: 22.8 us -> 21.2 us
  Pallas kernels: 9.22 us -> 10.5 us
  starting transfers between devices: 28.4 us -> 27.6 us
    ppermute x12, waiting for transfers between devices: 21.2 us -> 18.9 us  [shift(): return lax.ppermute(piece, 'amp', pairs)]
    pallas_call x10 -> x11, Pallas kernels: 9.22 us -> 10.5 us  [kernel(): pl.pallas_call(body, out_shape=out_shape, compiler_params=params, **{**sp...]
    ppermute x12, starting transfers between devices: 21.6 us -> 20.8 us  [shift(): return lax.ppermute(piece, 'amp', pairs)]
    ppermute x8, waiting for transfers between devices: 1.64 us -> 2.37 us  [swap(): return lax.ppermute(piece, axis, [(i, i ^ k) for i in range(size)])]
  transfers between devices with their start and end apart: 20 -> 20, of which waited for: 9 -> 7; matrix products, arithmetic and copies ran while one was open for 0% -> 0% of each run, Pallas kernels for 13% -> 15%
where the time goes in v4:
time: 61.9 us; the launch traced here: 61.2 us
  starting transfers between devices  27.6 us (45%)
  waiting for transfers between devices  21.2 us (34%)
  Pallas kernels  10.5 us (17%)
  local copies, waits for them, and re-layouts  1.1 us (2%)
  between operations  0.81 us (1%)
    ppermute x12, starting transfers between devices, shift(): return lax.ppermute(piece, 'amp', pairs)  20.8 us
    ppermute x12, waiting for transfers between devices, shift(): return lax.ppermute(piece, 'amp', pairs)  18.9 us
    pallas_call x11, Pallas kernels, kernel(): pl.pallas_call(body, out_shape=out_shape, compiler_params=params, **{**sp...  10.5 us
    ppermute x8, starting transfers between devices, swap(): return lax.ppermute(piece, axis, [(i, i ^ k) for i in range(size)])  6.77 us
    ppermute x8, waiting for transfers between devices, swap(): return lax.ppermute(piece, axis, [(i, i ^ k) for i in range(size)])  2.37 us
  transfers between devices with their start and end apart: 20, of which 7 were waited for; matrix products, arithmetic and copies ran while one was open for 0% of the time, Pallas kernels for 15%

profile of v4, /device:TPU:0, one launch (start us, length us, event | category | flops | bytes accessed | tf_op | source)
XLA Modules:
  0.0 61.2 jit_solution(1192494208483868323)
XLA Ops:
  0.6 1.1 %slice.4.x_ref = f32[128,8,128]{2,1,0:T(8,128)S(1)} slice(f32[128,16,128]{2,1,0:T(8,128)} %bitcast.9), slice={[0:128], [8:16], [0:128]} | slice | bytes 1048576 | tf_op jit(solution)/shard_map/slice | solution.py:312
  3.2 4.7 %collective-permute-start.2 = (f32[128,2,128]{2,1,0:T(2,128)S(1)}, f32[128,2,128]{2,1,0:T(2,128)S(1)}, u32[]{:S(2)}, u32[]{:S(2)}) collective-permute-start(f32[128,2,128]{2,1,0:T(2,128)S(1)} %shard_map.60), channel_id=1, source_target_pairs={{0,6},{1,7},{2,4},{3,5},{4,2},{5,3},{6,0},{7,1},{8,14},{9,15},{10,... | collective-permute-start | bytes 393224 | tf_op jit(solution)/shard_map/ppermute | solution.py:267
  7.9 1.1 %shard_map.59 = (f32[128,2,128]{2,1,0:T(2,128)S(1)}, f32[128,2,128]{2,1,0:T(2,128)S(1)}, f32[128,2,128]{2,1,0:T(2,128)S(1)}) custom-call(f32[128,8,2,128]{3,2,1,0:T(2,128)} %bitcast.11), custom_call_target="tpu_custom_call" | custom-call | tf_op jit(solution)/shard_map/pallas_call | solution.py:284
  9.6 2.6 %collective-permute-start.6 = (f32[3,128,128]{2,1,0:T(8,128)S(1)}, f32[3,128,128]{2,1,0:T(8,128)S(1)}, u32[]{:S(2)}, u32[]{:S(2)}) collective-permute-start(f32[3,128,128]{2,1,0:T(8,128)S(1)} %bitcast.5), channel_id=1, source_target_pairs={{0,24},{8,16},{16,8},{24,0},{1,25},{9,17},{17,9},{25,1},{2,26},{10... | collective-permute-start | bytes 589832 | tf_op jit(solution)/shard_map/ppermute | solution.py:260
  12.3 1.7 %collective-permute-start.5 = (f32[3,128,128]{2,1,0:T(8,128)S(1)}, f32[3,128,128]{2,1,0:T(8,128)S(1)}, u32[]{:S(2)}, u32[]{:S(2)}) collective-permute-start(f32[3,128,128]{2,1,0:T(8,128)S(1)} %bitcast.6), channel_id=1, source_target_pairs={{0,16},{8,24},{16,0},{24,8},{1,17},{9,25},{17,1},{25,9},{2,18},{10... | collective-permute-start | bytes 589832 | tf_op jit(solution)/shard_map/ppermute | solution.py:260
  14.0 1.9 %collective-permute-done.refs_1_ = f32[128,2,128]{2,1,0:T(2,128)S(1)} collective-permute-done((f32[128,2,128]{2,1,0:T(2,128)S(1)}, f32[128,2,128]{2,1,0:T(2,128)S(1)}, u32[]{:S(2)}, u32[]{:S(2)}) %collective-permute-start) | collective-permute-done | bytes 131104 | tf_op jit(solution)/shard_map/ppermute | solution.py:267
  15.9 3.7 %collective-permute-done.1.refs_2_ = f32[128,2,128]{2,1,0:T(2,128)S(1)} collective-permute-done((f32[128,2,128]{2,1,0:T(2,128)S(1)}, f32[128,2,128]{2,1,0:T(2,128)S(1)}, u32[]{:S(2)}, u32[]{:S(2)}) %collective-permute-start.1) | collective-permute-done | bytes 131104 | tf_op jit(solution)/shard_map/ppermute | solution.py:267
  20.2 1.6 %collective-permute-start.4 = (f32[3,128,128]{2,1,0:T(8,128)S(1)}, f32[3,128,128]{2,1,0:T(8,128)S(1)}, u32[]{:S(2)}, u32[]{:S(2)}) collective-permute-start(f32[3,128,128]{2,1,0:T(8,128)S(1)} %bitcast.7), channel_id=1, source_target_pairs={{0,8},{8,0},{16,24},{24,16},{1,9},{9,1},{17,25},{25,17},{2,10},{10... | collective-permute-start | bytes 589832 | tf_op jit(solution)/shard_map/ppermute | solution.py:260
  22.0 3.0 %collective-permute-start.13 = (f32[2,128,128]{2,1,0:T(8,128)S(1)}, f32[2,128,128]{2,1,0:T(8,128)S(1)}, u32[]{:S(2)}, u32[]{:S(2)}) collective-permute-start(f32[2,128,128]{2,1,0:T(8,128)S(1)} %get-tuple-element.45), channel_id=1, source_target_pairs={{0,4},{1,5},{2,6},{3,7},{4,0},{5,1},{6,2},{7,3},{8,12},{9,13},{10,... | collective-permute-start | bytes 393224 | tf_op jit(solution)/shard_map/ppermute | solution.py:267
  25.0 1.3 %collective-permute-start.14 = (f32[2,128,128]{2,1,0:T(8,128)S(1)}, f32[2,128,128]{2,1,0:T(8,128)S(1)}, u32[]{:S(2)}, u32[]{:S(2)}) collective-permute-start(f32[2,128,128]{2,1,0:T(8,128)S(1)} %get-tuple-element.46), channel_id=1, source_target_pairs={{0,6},{1,7},{2,4},{3,5},{4,2},{5,3},{6,0},{7,1},{8,14},{9,15},{10,... | collective-permute-start | bytes 393224 | tf_op jit(solution)/shard_map/ppermute | solution.py:267
  26.3 1.1 %collective-permute-done.4.refs_1_ = f32[3,128,128]{2,1,0:T(8,128)S(1)} collective-permute-done((f32[3,128,128]{2,1,0:T(8,128)S(1)}, f32[3,128,128]{2,1,0:T(8,128)S(1)}, u32[]{:S(2)}, u32[]{:S(2)}) %collective-permute-start.4) | collective-permute-done | bytes 196640 | tf_op jit(solution)/shard_map/ppermute | solution.py:260
  27.5 2.0 %shard_map.62 = (bf16[4,256,256]{2,1,0:T(8,128)(2,1)S(1)}, bf16[4,256,256]{2,1,0:T(8,128)(2,1)S(1)}) custom-call(s32[4,3,7]{2,1,0:T(4,128)S(1)} %copy.6.picks_ref, s32[4,3]{1,0:T(4,128)S(1)} %copy-done.1, f32[3,128,128]{2,1,0:T(8,128)S(1)} %bitcast.8, f32[3,128,128]{2,1,0:T(8,128)S(1)} %collective-permute-done.4.refs_1_, ...), custom_call_target="tpu_custom_call" | custom-call | tf_op jit(solution)/shard_map/pallas_call | solution.py:284
  29.5 2.3 %shard_map.63 = (f32[2,128,128]{2,1,0:T(8,128)S(1)}, f32[2,128,128]{2,1,0:T(8,128)S(1)}, f32[2,128,128]{2,1,0:T(8,128)S(1)}, f32[2,128,128]{2,1,0:T(8,128)S(1)}, f32[8,128]{1,0:T(8,128)S(1)}) custom-call(f32[4,128,128]{2,1,0:T(8,128)S(1)} %get-tuple-element.33.refs_0_, f32[4,128,128]{2,1,0:T(8,128)S(1)} %collective-permute-done.3.refs_1_, ...), custom_call_target="tpu_custom_call" | custom-call | tf_op jit(solution)/shard_map/pallas_call | solution.py:284
  31.9 3.0 %collective-permute-start.8 = (f32[2,128,128]{2,1,0:T(8,128)S(1)}, f32[2,128,128]{2,1,0:T(8,128)S(1)}, u32[]{:S(2)}, u32[]{:S(2)}) collective-permute-start(f32[2,128,128]{2,1,0:T(8,128)S(1)} %get-tuple-element.39), channel_id=1, source_target_pairs={{0,4},{1,5},{2,6},{3,7},{4,0},{5,1},{6,2},{7,3},{8,12},{9,13},{10,... | collective-permute-start | bytes 393224 | tf_op jit(solution)/shard_map/ppermute | solution.py:267
  34.9 1.3 %collective-permute-start.9 = (f32[2,128,128]{2,1,0:T(8,128)S(1)}, f32[2,128,128]{2,1,0:T(8,128)S(1)}, u32[]{:S(2)}, u32[]{:S(2)}) collective-permute-start(f32[2,128,128]{2,1,0:T(8,128)S(1)} %get-tuple-element.40), channel_id=1, source_target_pairs={{0,6},{1,7},{2,4},{3,5},{4,2},{5,3},{6,0},{7,1},{8,14},{9,15},{10,... | collective-permute-start | bytes 393224 | tf_op jit(solution)/shard_map/ppermute | solution.py:267
  36.3 2.3 %shard_map.66 = (f32[264,128]{1,0:T(8,128)S(1)}, f32[392,128]{1,0:T(8,128)S(1)}, f32[392,128]{1,0:T(8,128)S(1)}) custom-call(f32[2,128,128]{2,1,0:T(8,128)S(1)} %get-tuple-element.43.refs_0_, f32[2,128,128]{2,1,0:T(8,128)S(1)} %collective-permute-done.12.refs_1_, f32[2,128,128]{2,1,0:T(8,128)S(1)} %collective-permute-done.13.refs_2_, ...), custom_call_target="tpu_custom_call" | custom-call | tf_op jit(solution)/shard_map/pallas_call | solution.py:284
  38.7 7.5 %collective-permute-done.8.refs_2_ = f32[2,128,128]{2,1,0:T(8,128)S(1)} collective-permute-done((f32[2,128,128]{2,1,0:T(8,128)S(1)}, f32[2,128,128]{2,1,0:T(8,128)S(1)}, u32[]{:S(2)}, u32[]{:S(2)}) %collective-permute-start.8) | collective-permute-done | bytes 131104 | tf_op jit(solution)/shard_map/ppermute | solution.py:267
  46.4 2.6 %collective-permute-start.18 = (f32[264,128]{1,0:T(8,128)S(1)}, f32[264,128]{1,0:T(8,128)S(1)}, u32[]{:S(2)}, u32[]{:S(2)}) collective-permute-start(f32[264,128]{1,0:T(8,128)S(1)} %get-tuple-element.53), channel_id=1, source_target_pairs={{0,2},{1,3},{2,4},{3,5},{4,6},{5,7},{6,0},{7,1},{8,10},{9,11},{10,... | collective-permute-start | bytes 405512 | tf_op jit(solution)/shard_map/ppermute | solution.py:267
  49.0 1.1 %collective-permute-start.16 = (f32[264,128]{1,0:T(8,128)S(1)}, f32[264,128]{1,0:T(8,128)S(1)}, u32[]{:S(2)}, u32[]{:S(2)}) collective-permute-start(f32[264,128]{1,0:T(8,128)S(1)} %get-tuple-element.51), channel_id=1, source_target_pairs={{0,4},{1,5},{2,6},{3,7},{4,0},{5,1},{6,2},{7,3},{8,12},{9,13},{10,... | collective-permute-start | bytes 405512 | tf_op jit(solution)/shard_map/ppermute | solution.py:267
  50.1 2.9 %collective-permute-start.17 = (f32[264,128]{1,0:T(8,128)S(1)}, f32[264,128]{1,0:T(8,128)S(1)}, u32[]{:S(2)}, u32[]{:S(2)}) collective-permute-start(f32[264,128]{1,0:T(8,128)S(1)} %get-tuple-element.52), channel_id=1, source_target_pairs={{0,6},{1,7},{2,0},{3,1},{4,2},{5,3},{6,4},{7,5},{8,14},{9,15},{10,... | collective-permute-start | bytes 405512 | tf_op jit(solution)/shard_map/ppermute | solution.py:267
  53.0 1.7 %collective-permute-done.18.piece_ref = f32[264,128]{1,0:T(8,128)S(1)} collective-permute-done((f32[264,128]{1,0:T(8,128)S(1)}, f32[264,128]{1,0:T(8,128)S(1)}, u32[]{:S(2)}, u32[]{:S(2)}) %collective-permute-start.18) | collective-permute-done | bytes 135200 | tf_op jit(solution)/shard_map/ppermute | solution.py:267
  54.8 1.2 %collective-permute-done.19.refs_6_ = f32[136,128]{1,0:T(8,128)S(1)} collective-permute-done((f32[136,128]{1,0:T(8,128)S(1)}, f32[136,128]{1,0:T(8,128)S(1)}, u32[]{:S(2)}, u32[]{:S(2)}) %collective-permute-start.19) | collective-permute-done | bytes 69664 | tf_op jit(solution)/shard_map/ppermute | solution.py:260
  56.0 4.0 %collective-permute-done.16.refs_3_ = f32[264,128]{1,0:T(8,128)S(1)} collective-permute-done((f32[264,128]{1,0:T(8,128)S(1)}, f32[264,128]{1,0:T(8,128)S(1)}, u32[]{:S(2)}, u32[]{:S(2)}) %collective-permute-start.16) | collective-permute-done | bytes 135200 | tf_op jit(solution)/shard_map/ppermute | solution.py:267
  60.0 1.2 %shard_map.69 = (f32[128,16,128]{2,1,0:T(8,128)}, f32[1,4]{1,0:T(1,128)}) custom-call(f32[4,128,128]{2,1,0:T(8,128)S(1)} %get-tuple-element.41.refs_0_, f32[4,128,128]{2,1,0:T(8,128)S(1)} %collective-permute-done.10.refs_1_, f32[264,128]{1,0:T(8,128)S(1)} %get-tuple-element.50.refs_2_, f32[264,128]{1,0:T(8,128)S(1)} %collective-permute-done.16.refs_3_, ...), custom_call_target="tpu_custom_call" | custom-call | tf_op jit(solution)/shard_map/pallas_call | solution.py:284
  (35 shorter events, 3.3 us)
Async XLA Ops:
  1.7 20.0 %collective-permute-start.11 = (f32[128,8,128]{2,1,0:T(8,128)S(1)}, f32[128,8,128]{2,1,0:T(8,128)S(1)}, u32[]{:S(2)}, u32[]{:S(2)}) collective-permute-start(f32[128,8,128]{2,1,0:T(8,128)S(1)} %slice.4.x_ref), channel_id=1, source_target_pairs={{0,1},{1,0},{2,3},{3,2},{4,5},{5,4},{6,7},{7,6},{8,9},{9,8},{10,11... | collective-permute-start | bytes 1572872 | tf_op jit(solution)/shard_map/ppermute | solution.py:260
  3.2 6.4 %copy-start = (f32[1,3,128,128]{3,2,1,0:T(8,128)S(1)}, f32[1,3,128,128]{3,2,1,0:T(8,128)}, u32[]{:S(2)}) copy-start(f32[1,3,128,128]{3,2,1,0:T(8,128)} %param.5) | copy-start | bytes 589828
  3.2 9.1 %collective-permute-start.2 = (f32[128,2,128]{2,1,0:T(2,128)S(1)}, f32[128,2,128]{2,1,0:T(2,128)S(1)}, u32[]{:S(2)}, u32[]{:S(2)}) collective-permute-start(f32[128,2,128]{2,1,0:T(2,128)S(1)} %shard_map.60), channel_id=1, source_target_pairs={{0,6},{1,7},{2,4},{3,5},{4,2},{5,3},{6,0},{7,1},{8,14},{9,15},{10,... | collective-permute-start | bytes 393224 | tf_op jit(solution)/shard_map/ppermute | solution.py:267
  9.0 7.0 %collective-permute-start = (f32[128,2,128]{2,1,0:T(2,128)S(1)}, f32[128,2,128]{2,1,0:T(2,128)S(1)}, u32[]{:S(2)}, u32[]{:S(2)}) collective-permute-start(f32[128,2,128]{2,1,0:T(2,128)S(1)} %get-tuple-element.31), channel_id=1, source_target_pairs={{0,2},{1,3},{2,0},{3,1},{4,6},{5,7},{6,4},{7,5},{8,10},{9,11},{10,... | collective-permute-start | bytes 393224 | tf_op jit(solution)/shard_map/ppermute | solution.py:267
  9.0 10.6 %collective-permute-start.1 = (f32[128,2,128]{2,1,0:T(2,128)S(1)}, f32[128,2,128]{2,1,0:T(2,128)S(1)}, u32[]{:S(2)}, u32[]{:S(2)}) collective-permute-start(f32[128,2,128]{2,1,0:T(2,128)S(1)} %get-tuple-element.32), channel_id=1, source_target_pairs={{0,4},{1,5},{2,6},{3,7},{4,0},{5,1},{6,2},{7,3},{8,12},{9,13},{10,... | collective-permute-start | bytes 393224 | tf_op jit(solution)/shard_map/ppermute | solution.py:267
  9.6 12.3 %collective-permute-start.6 = (f32[3,128,128]{2,1,0:T(8,128)S(1)}, f32[3,128,128]{2,1,0:T(8,128)S(1)}, u32[]{:S(2)}, u32[]{:S(2)}) collective-permute-start(f32[3,128,128]{2,1,0:T(8,128)S(1)} %bitcast.5), channel_id=1, source_target_pairs={{0,24},{8,16},{16,8},{24,0},{1,25},{9,17},{17,9},{25,1},{2,26},{10... | collective-permute-start | bytes 589832 | tf_op jit(solution)/shard_map/ppermute | solution.py:260
  12.3 12.7 %collective-permute-start.5 = (f32[3,128,128]{2,1,0:T(8,128)S(1)}, f32[3,128,128]{2,1,0:T(8,128)S(1)}, u32[]{:S(2)}, u32[]{:S(2)}) collective-permute-start(f32[3,128,128]{2,1,0:T(8,128)S(1)} %bitcast.6), channel_id=1, source_target_pairs={{0,16},{8,24},{16,0},{24,8},{1,17},{9,25},{17,1},{25,9},{2,18},{10... | collective-permute-start | bytes 589832 | tf_op jit(solution)/shard_map/ppermute | solution.py:260
  20.1 9.4 %collective-permute-start.3 = (f32[4,128,128]{2,1,0:T(8,128)S(1)}, f32[4,128,128]{2,1,0:T(8,128)S(1)}, u32[]{:S(2)}, u32[]{:S(2)}) collective-permute-start(f32[4,128,128]{2,1,0:T(8,128)S(1)} %get-tuple-element.34), channel_id=1, source_target_pairs={{0,1},{1,0},{2,3},{3,2},{4,5},{5,4},{6,7},{7,6},{8,9},{9,8},{10,11... | collective-permute-start | bytes 786440 | tf_op jit(solution)/shard_map/ppermute | solution.py:260
  20.2 7.3 %collective-permute-start.4 = (f32[3,128,128]{2,1,0:T(8,128)S(1)}, f32[3,128,128]{2,1,0:T(8,128)S(1)}, u32[]{:S(2)}, u32[]{:S(2)}) collective-permute-start(f32[3,128,128]{2,1,0:T(8,128)S(1)} %bitcast.7), channel_id=1, source_target_pairs={{0,8},{8,0},{16,24},{24,16},{1,9},{9,1},{17,25},{25,17},{2,10},{10... | collective-permute-start | bytes 589832 | tf_op jit(solution)/shard_map/ppermute | solution.py:260
  21.9 4.5 %copy-start.2 = (s32[1,4,3,7]{3,1,2,0:T(4,128)S(1)}, s32[1,4,3,7]{3,1,2,0:T(4,128)}, u32[]{:S(2)}) copy-start(s32[1,4,3,7]{3,1,2,0:T(4,128)} %param.6) | copy-start | bytes 1012
  21.9 13.0 %collective-permute-start.12 = (f32[2,128,128]{2,1,0:T(8,128)S(1)}, f32[2,128,128]{2,1,0:T(8,128)S(1)}, u32[]{:S(2)}, u32[]{:S(2)}) collective-permute-start(f32[2,128,128]{2,1,0:T(8,128)S(1)} %get-tuple-element.44), channel_id=1, source_target_pairs={{0,2},{1,3},{2,0},{3,1},{4,6},{5,7},{6,4},{7,5},{8,10},{9,11},{10,... | collective-permute-start | bytes 393224 | tf_op jit(solution)/shard_map/ppermute | solution.py:267
  22.0 14.3 %collective-permute-start.13 = (f32[2,128,128]{2,1,0:T(8,128)S(1)}, f32[2,128,128]{2,1,0:T(8,128)S(1)}, u32[]{:S(2)}, u32[]{:S(2)}) collective-permute-start(f32[2,128,128]{2,1,0:T(8,128)S(1)} %get-tuple-element.45), channel_id=1, source_target_pairs={{0,4},{1,5},{2,6},{3,7},{4,0},{5,1},{6,2},{7,3},{8,12},{9,13},{10,... | collective-permute-start | bytes 393224 | tf_op jit(solution)/shard_map/ppermute | solution.py:267
  25.0 11.3 %collective-permute-start.14 = (f32[2,128,128]{2,1,0:T(8,128)S(1)}, f32[2,128,128]{2,1,0:T(8,128)S(1)}, u32[]{:S(2)}, u32[]{:S(2)}) collective-permute-start(f32[2,128,128]{2,1,0:T(8,128)S(1)} %get-tuple-element.46), channel_id=1, source_target_pairs={{0,6},{1,7},{2,4},{3,5},{4,2},{5,3},{6,0},{7,1},{8,14},{9,15},{10,... | collective-permute-start | bytes 393224 | tf_op jit(solution)/shard_map/ppermute | solution.py:267
  26.3 1.1 %copy-start.1 = (s32[4,3]{1,0:T(4,128)S(1)}, s32[4,3]{1,0:T(4,128)}, u32[]{:S(2)}) copy-start(s32[4,3]{1,0:T(4,128)} %targets_ref.1) | copy-start | bytes 148
  31.8 6.9 %collective-permute-start.7 = (f32[2,128,128]{2,1,0:T(8,128)S(1)}, f32[2,128,128]{2,1,0:T(8,128)S(1)}, u32[]{:S(2)}, u32[]{:S(2)}) collective-permute-start(f32[2,128,128]{2,1,0:T(8,128)S(1)} %get-tuple-element.38), channel_id=1, source_target_pairs={{0,2},{1,3},{2,0},{3,1},{4,6},{5,7},{6,4},{7,5},{8,10},{9,11},{10,... | collective-permute-start | bytes 393224 | tf_op jit(solution)/shard_map/ppermute | solution.py:267
  31.9 14.3 %collective-permute-start.8 = (f32[2,128,128]{2,1,0:T(8,128)S(1)}, f32[2,128,128]{2,1,0:T(8,128)S(1)}, u32[]{:S(2)}, u32[]{:S(2)}) collective-permute-start(f32[2,128,128]{2,1,0:T(8,128)S(1)} %get-tuple-element.39), channel_id=1, source_target_pairs={{0,4},{1,5},{2,6},{3,7},{4,0},{5,1},{6,2},{7,3},{8,12},{9,13},{10,... | collective-permute-start | bytes 393224 | tf_op jit(solution)/shard_map/ppermute | solution.py:267
  34.9 11.3 %collective-permute-start.9 = (f32[2,128,128]{2,1,0:T(8,128)S(1)}, f32[2,128,128]{2,1,0:T(8,128)S(1)}, u32[]{:S(2)}, u32[]{:S(2)}) collective-permute-start(f32[2,128,128]{2,1,0:T(8,128)S(1)} %get-tuple-element.40), channel_id=1, source_target_pairs={{0,6},{1,7},{2,4},{3,5},{4,2},{5,3},{6,0},{7,1},{8,14},{9,15},{10,... | collective-permute-start | bytes 393224 | tf_op jit(solution)/shard_map/ppermute | solution.py:267
  38.6 10.4 %collective-permute-start.15 = (f32[392,128]{1,0:T(8,128)S(1)}, f32[392,128]{1,0:T(8,128)S(1)}, u32[]{:S(2)}, u32[]{:S(2)}) collective-permute-start(f32[392,128]{1,0:T(8,128)S(1)} %get-tuple-element.49), channel_id=1, source_target_pairs={{0,1},{1,0},{2,3},{3,2},{4,5},{5,4},{6,7},{7,6},{8,9},{9,8},{10,11... | collective-permute-start | bytes 602120 | tf_op jit(solution)/shard_map/ppermute | solution.py:260
  46.3 8.5 %collective-permute-start.10 = (f32[4,128,128]{2,1,0:T(8,128)S(1)}, f32[4,128,128]{2,1,0:T(8,128)S(1)}, u32[]{:S(2)}, u32[]{:S(2)}) collective-permute-start(f32[4,128,128]{2,1,0:T(8,128)S(1)} %get-tuple-element.42), channel_id=1, source_target_pairs={{0,1},{1,0},{2,3},{3,2},{4,5},{5,4},{6,7},{7,6},{8,9},{9,8},{10,11... | collective-permute-start | bytes 786440 | tf_op jit(solution)/shard_map/ppermute | solution.py:260
  46.4 8.3 %collective-permute-start.18 = (f32[264,128]{1,0:T(8,128)S(1)}, f32[264,128]{1,0:T(8,128)S(1)}, u32[]{:S(2)}, u32[]{:S(2)}) collective-permute-start(f32[264,128]{1,0:T(8,128)S(1)} %get-tuple-element.53), channel_id=1, source_target_pairs={{0,2},{1,3},{2,4},{3,5},{4,6},{5,7},{6,0},{7,1},{8,10},{9,11},{10,... | collective-permute-start | bytes 405512 | tf_op jit(solution)/shard_map/ppermute | solution.py:267
  49.0 11.0 %collective-permute-start.16 = (f32[264,128]{1,0:T(8,128)S(1)}, f32[264,128]{1,0:T(8,128)S(1)}, u32[]{:S(2)}, u32[]{:S(2)}) collective-permute-start(f32[264,128]{1,0:T(8,128)S(1)} %get-tuple-element.51), channel_id=1, source_target_pairs={{0,4},{1,5},{2,6},{3,7},{4,0},{5,1},{6,2},{7,3},{8,12},{9,13},{10,... | collective-permute-start | bytes 405512 | tf_op jit(solution)/shard_map/ppermute | solution.py:267
  50.1 9.9 %collective-permute-start.17 = (f32[264,128]{1,0:T(8,128)S(1)}, f32[264,128]{1,0:T(8,128)S(1)}, u32[]{:S(2)}, u32[]{:S(2)}) collective-permute-start(f32[264,128]{1,0:T(8,128)S(1)} %get-tuple-element.52), channel_id=1, source_target_pairs={{0,6},{1,7},{2,0},{3,1},{4,2},{5,3},{6,4},{7,5},{8,14},{9,15},{10,... | collective-permute-start | bytes 405512 | tf_op jit(solution)/shard_map/ppermute | solution.py:267
  54.7 1.3 %collective-permute-start.19 = (f32[136,128]{1,0:T(8,128)S(1)}, f32[136,128]{1,0:T(8,128)S(1)}, u32[]{:S(2)}, u32[]{:S(2)}) collective-permute-start(f32[136,128]{1,0:T(8,128)S(1)} %get-tuple-element.55), channel_id=1, source_target_pairs={{0,1},{1,0},{2,3},{3,2},{4,5},{5,4},{6,7},{7,6},{8,9},{9,8},{10,11... | collective-permute-start | bytes 208904 | tf_op jit(solution)/shard_map/ppermute | solution.py:260
